TPU v7x, 128 devices: a whole 4x4x4 slice. The times are simulated.
128 devices in a mesh: lat: 8 (over y, z_lo), lon: 16 (over x, z_hi, core).
Axes of the slice: x: 4, y: 4, z: 4 (z_hi: 2, z_lo: 2; z = z_hi * 2 + z_lo), core: 2. Of those that a mesh axis runs over, the one named last changes fastest.
Arguments:
- x_first: bfloat16 [4, 48, 192, 512], P(None, 'lat', 'lon'), may hold values from -6 to 6
- x_second: bfloat16 [4, 48, 192, 512], P(None, 'lat', 'lon'), may hold values from -6 to 6
- cotangent: bfloat16 [4, 48, 192, 512], P(None, 'lat', 'lon'), may hold values from -6 to 6
- w_attn_in: bfloat16 [2, 512, 1536], replicated, may hold values from -0.25 to 0.25
- w_attn_out: bfloat16 [2, 512, 512], replicated, may hold values from -0.25 to 0.25
- w_up: bfloat16 [2, 512, 2048], replicated, may hold values from -0.25 to 0.25
- w_down: bfloat16 [2, 2048, 512], replicated, may hold values from -0.125 to 0.125
- norm_gains: float32 [2, 2, 512], replicated, may hold values from 0.1 to 1.9
- logit_scales: float32 [2, 8], replicated, may hold values from 2 to 30
Outputs:
- grad_first: float32 [4, 48, 192, 512], P(None, 'lat', 'lon')
- grad_second: float32 [4, 48, 192, 512], P(None, 'lat', 'lon')
All inputs are finite; a program needn't handle non-finite values.
Results may differ from a plain program's by a relative error of at most 0.022.
Values may be sent and summed in bfloat16 or wider, within the bound.
A program may use at most 192 MiB of HBM per device.

v0:
```python
import jax
import jax.numpy as jnp
from jax import lax
from jax.sharding import PartitionSpec as P

WIN_LEV = 2
WIN_LAT = 6
WIN_LON = 12


EPSILON = 1e-05


def passed_along(value, axis, steps):
    count = lax.axis_size(axis)
    pairs = [(source, (source + steps) % count) for source in range(count)]
    return lax.ppermute(value, axis, pairs)


def as_sent(array):
    return jax.tree.map(lambda a: a.astype(jnp.bfloat16) if a.dtype == jnp.float32 else a, array)


def layer_norm(tokens_in, gain_vector):
    center = tokens_in - jnp.mean(tokens_in, axis=-1, keepdims=True)
    spread = jnp.mean(center * center, axis=-1, keepdims=True)
    return center * lax.rsqrt(spread + EPSILON) * gain_vector


def unit_rows(vectors):
    return vectors * lax.rsqrt(jnp.sum(vectors * vectors, axis=-1, keepdims=True) + 1e-06)


def swin_block(windows, labels, w_in, w_out, w_upper, w_lower, gains, scales):
    window_count, length, feature_width = windows.shape
    head_count = scales.shape[0]
    head_size = feature_width // head_count
    normed = layer_norm(windows, gains[0]).astype(jnp.bfloat16)
    projected = jnp.dot(
        normed.reshape(window_count * length, feature_width),
        w_in,
        preferred_element_type=jnp.float32,
    )
    projected = projected.reshape(window_count, length, 3, head_count, head_size)
    queries = unit_rows(projected[:, :, 0]).astype(jnp.bfloat16)
    key_rows = unit_rows(projected[:, :, 1]).astype(jnp.bfloat16)
    values = projected[:, :, 2].astype(jnp.bfloat16)
    scores = (
        jnp.einsum("wqhc,wkhc->whqk", queries, key_rows, preferred_element_type=jnp.float32)
        * scales[None, :, None, None]
    )
    allowed = (labels[:, :, None] == labels[:, None, :])[:, None]
    weights = jnp.where(allowed, jnp.exp(scores), 0.0)
    probabilities = (weights / jnp.sum(weights, axis=-1, keepdims=True)).astype(jnp.bfloat16)
    mixture = jnp.einsum(
        "whqk,wkhc->wqhc", probabilities, values, preferred_element_type=jnp.float32
    ).astype(jnp.bfloat16)
    attended = jnp.dot(
        mixture.reshape(window_count * length, feature_width),
        w_out,
        preferred_element_type=jnp.float32,
    )
    residual_mid = windows + attended.reshape(window_count, length, feature_width)
    normed_two = layer_norm(residual_mid, gains[1]).astype(jnp.bfloat16)
    hidden = jax.nn.gelu(
        jnp.dot(
            normed_two.reshape(window_count * length, feature_width),
            w_upper,
            preferred_element_type=jnp.float32,
        )
    ).astype(jnp.bfloat16)
    lowered = jnp.dot(hidden, w_lower, preferred_element_type=jnp.float32)
    return residual_mid + lowered.reshape(window_count, length, feature_width)


def to_windows(lattice):
    level_count, row_count, col_count = lattice.shape[:3]
    trailing = lattice.shape[3:]
    blocked = lattice.reshape(
        (
            level_count // WIN_LEV,
            WIN_LEV,
            row_count // WIN_LAT,
            WIN_LAT,
            col_count // WIN_LON,
            WIN_LON,
        )
        + trailing
    )
    axis_order = (0, 2, 4, 1, 3, 5) + tuple(range(6, 6 + len(trailing)))
    return blocked.transpose(axis_order).reshape((-1, WIN_LEV * WIN_LAT * WIN_LON) + trailing)


def from_windows(windows, level_count, row_count, col_count):
    trailing = windows.shape[2:]
    blocked = windows.reshape(
        (
            level_count // WIN_LEV,
            row_count // WIN_LAT,
            col_count // WIN_LON,
            WIN_LEV,
            WIN_LAT,
            WIN_LON,
        )
        + trailing
    )
    axis_order = (0, 3, 1, 4, 2, 5) + tuple(range(6, 6 + len(trailing)))
    return blocked.transpose(axis_order).reshape((level_count, row_count, col_count) + trailing)


def region_labels(level_count, row_start, row_count, total_rows, col_count):
    level_ids = jnp.arange(level_count, dtype=jnp.int32)
    level_part = (level_ids >= level_count - WIN_LEV).astype(jnp.int32) + (
        level_ids >= level_count - WIN_LEV // 2
    ).astype(jnp.int32)
    row_ids = jnp.mod(row_start + jnp.arange(row_count, dtype=jnp.int32), total_rows)
    row_part = (row_ids >= total_rows - WIN_LAT).astype(jnp.int32) + (
        row_ids >= total_rows - WIN_LAT // 2
    ).astype(jnp.int32)
    return jnp.broadcast_to(
        level_part[:, None, None] * 3 + row_part[None, :, None], (level_count, row_count, col_count)
    )


def tile_block(
    lattice, labels, w_attn_in, w_attn_out, w_up, w_down, norm_gains, logit_scales, block_index
):
    result = swin_block(
        to_windows(lattice),
        to_windows(labels),
        w_attn_in[block_index],
        w_attn_out[block_index],
        w_up[block_index],
        w_down[block_index],
        norm_gains[block_index],
        logit_scales[block_index],
    )
    return from_windows(result, lattice.shape[0], lattice.shape[1], lattice.shape[2])


def rows_ahead(rim_pair):
    half_rows = WIN_LAT // 2
    coming = passed_along((rim_pair[0][:, :half_rows], rim_pair[1][:, :half_rows]), "lat", -1)
    return (
        jnp.concatenate([rim_pair[0][:, half_rows:], coming[0]], axis=1),
        jnp.concatenate([rim_pair[1][:, half_rows:], coming[1]], axis=1),
    )


def cols_ahead(rim_pair):
    half_cols = WIN_LON // 2
    coming = passed_along((rim_pair[0][:, :, :half_cols], rim_pair[1][:, :, :half_cols]), "lon", -1)
    return (
        jnp.concatenate([rim_pair[0][:, :, half_cols:], coming[0]], axis=2),
        jnp.concatenate([rim_pair[1][:, :, half_cols:], coming[1]], axis=2),
    )


def rows_behind(gradient):
    row_count = gradient.shape[1]
    keep_rows = row_count - WIN_LAT // 2
    coming = passed_along(as_sent(gradient[:, keep_rows:]), "lat", 1)
    return jnp.concatenate([coming, gradient[:, :keep_rows]], axis=1)


def cols_behind(gradient):
    col_count = gradient.shape[2]
    keep_cols = col_count - WIN_LON // 2
    coming = passed_along(gradient[:, :, keep_cols:].astype(jnp.bfloat16), "lon", 1).astype(
        jnp.float32
    )
    return jnp.concatenate([coming, gradient[:, :, :keep_cols]], axis=2)


def per_device(
    x_first, x_second, cotangent, w_attn_in, w_attn_out, w_up, w_down, norm_gains, logit_scales
):
    level_count, row_count, col_count = x_first.shape[:3]
    total_rows = lax.axis_size("lat") * row_count
    row_start = lax.axis_index("lat") * row_count
    labels_one = jnp.zeros((level_count, row_count, col_count), jnp.int32)

    def second_with(labels_two):

        def second_block(lattice):
            return tile_block(
                lattice,
                labels_two,
                w_attn_in,
                w_attn_out,
                w_up,
                w_down,
                norm_gains,
                logit_scales,
                1,
            )

        return second_block

    def first_block(lattice):
        return tile_block(
            lattice, labels_one, w_attn_in, w_attn_out, w_up, w_down, norm_gains, logit_scales, 0
        )

    rim_pair = cols_ahead(rows_ahead((x_second, cotangent)))
    rolled_input = jnp.roll(rim_pair[0], -(WIN_LEV // 2), axis=0).astype(jnp.float32)
    rolled_cot = jnp.roll(rim_pair[1], -(WIN_LEV // 2), axis=0).astype(jnp.float32)
    labels_two = region_labels(level_count, row_start, row_count, total_rows, col_count)
    unused_two, pullback_two = jax.vjp(second_with(labels_two), rolled_input)
    grad_rolled = jnp.roll(pullback_two(rolled_cot)[0], WIN_LEV // 2, axis=0)
    grad_second = rows_behind(cols_behind(grad_rolled))
    unused_one, pullback_one = jax.vjp(first_block, x_first.astype(jnp.float32))
    grad_first = pullback_one(grad_second)[0]
    return (grad_first, grad_second)


def solution(mesh):
    placed = (
        P(None, "lat", "lon", None),
        P(None, "lat", "lon", None),
        P(None, "lat", "lon", None),
        P(),
        P(),
        P(),
        P(),
        P(),
        P(),
    )
    return jax.shard_map(
        per_device,
        mesh=mesh,
        in_specs=placed,
        out_specs=(P(None, "lat", "lon", None), P(None, "lat", "lon", None)),
        check_vma=False,
    )
```

profile of v0, /device:TPU:0, one launch (start us, length us, event | category | flops | bytes accessed | tf_op | source)
XLA Modules:
  0.0 167.3 jit_solution(1908549919638678720)
XLA Ops:
  0.7 1.8 %fusion.200 = (bf16[4,3,12,512]{3,0,2,1:T(4,128)(2,1)}, bf16[4,3,12,512]{3,0,2,1:T(4,128)(2,1)}) fusion(bf16[4,6,12,512]{3,0,2,1:T(4,128)(2,1)} %param.11), kind=kLoop, calls=%fused_computation.285 | loop fusion | bytes 589824 | tf_op jit(solution)/shard_map/slice | solution.py:146
  2.5 4.5 %collective-permute-start = (bf16[4,3,12,512]{3,0,2,1:T(4,128)(2,1)}, bf16[4,3,12,512]{3,0,2,1:T(4,128)(2,1)}, u32[]{:S(2)}, u32[]{:S(2)}) collective-permute-start(bf16[4,3,12,512]{3,0,2,1:T(4,128)(2,1)} %get-tuple-element.37), channel_id=1, source_target_pairs={{0,112},{16,0},{32,16},{48,32},{64,48},{80,64},{96,80},{112,96},{1... | collective-permute-start | bytes 442376 | tf_op jit(solution)/shard_map/ppermute | solution.py:17
  7.0 1.8 %fusion.199 = (bf16[4,3,12,512]{3,0,2,1:T(4,128)(2,1)}, bf16[4,3,12,512]{3,0,2,1:T(4,128)(2,1)}) fusion(bf16[4,6,12,512]{3,0,2,1:T(4,128)(2,1)} %param.10), kind=kLoop, calls=%fused_computation.284 | loop fusion | bytes 589824 | tf_op jit(solution)/shard_map/slice | solution.py:145
  8.9 1.1 copy_convert_fusion
  11.7 3.8 %slice_bitcast_fusion = (bf16[1536,512]{0,1:T(8,128)(2,1)}, bf16[1536,512]{0,1:T(8,128)(2,1)}) fusion(bf16[2,512,1536]{2,1,0:T(8,128)(2,1)} %param.12), kind=kLoop, calls=%fused_computation.87 | loop fusion | bytes 6291456 | tf_op jit(solution)/shard_map/jvp()/dot_general | solution.py:39
  16.2 1.9 %copy.177 = bf16[1536,512]{1,0:T(8,128)(2,1)S(1)} copy(bf16[1536,512]{0,1:T(8,128)(2,1)} %get-tuple-element.26) | data formatting | bytes 3145728 | tf_op jit(solution)/shard_map/jvp()/dot_general | solution.py:39
  19.0 1.0 multiply_convert_fusion.4
  20.0 1.1 reshape.528
  21.0 1.0 fusion.160
  25.7 0.8 copy-done.2
  26.8 1.1 fusion.171
  27.9 5.0 %collective-permute-start.1 = (bf16[4,6,6,512]{3,0,2,1:T(4,128)(2,1)S(1)}, bf16[4,6,6,512]{3,0,2,1:T(4,128)(2,1)S(1)}, u32[]{:S(2)}, u32[]{:S(2)}) collective-permute-start(bf16[4,6,6,512]{3,0,2,1:T(4,128)(2,1)S(1)} %get-tuple-element.35), channel_id=1, source_target_pairs={{0,15},{1,0},{2,1},{3,2},{4,3},{5,4},{6,5},{7,6},{8,7},{9,8},{10,9... | collective-permute-start | bytes 442376 | tf_op jit(solution)/shard_map/ppermute | solution.py:17
  33.5 0.9 reshape.515
  37.1 1.6 copy.157
  38.7 1.1 fusion.170
  39.8 1.6 collective-permute-start.3
  42.2 1.9 %collective-permute-done.3 = bf16[4,6,6,512]{3,0,2,1:T(4,128)(2,1)S(1)} collective-permute-done((bf16[4,6,6,512]{3,0,2,1:T(4,128)(2,1)S(1)}, bf16[4,6,6,512]{3,0,2,1:T(4,128)(2,1)S(1)}, u32[]{:S(2)}, u32[]{:S(2)}) %collective-permute-start.3) | collective-permute-done | bytes 147488 | tf_op jit(solution)/shard_map/ppermute | solution.py:17
  44.9 0.9 reshape.518
  45.8 0.9 reshape.521
  50.0 0.9 reshape.517
  50.9 0.8 reshape.502
  52.1 0.8 reshape.525
  52.9 2.5 %fusion.162 = f32[2,144,3,8,64]{1,4,3,2,0:T(8,128)S(1)} fusion(bf16[3,8,64,512,1]{3,2,1,0,4:T(8,128)(2,1)} %bitcast.230, bf16[2,144,512,1,1]{2,1,0,3,4:T(8,128)(2,1)} %reshape.525), kind=kOutput, calls=%fused_computation.218 | convolution fusion | flops 452984832 | bytes 3637248 | tf_op jit(solution)/shard_map/jvp()/dot_general | solution.py:39
  56.3 0.9 fusion.78
  60.2 1.3 copy-done.73
  61.6 1.8 %convolution_convert_fusion.1 = bf16[288,2048]{1,0:T(8,128)(2,1)} fusion(bf16[288,512]{1,0:T(8,128)(2,1)S(1)} %copy-done.31, bf16[2,2048,512]{2,1,0:T(8,128)(2,1)S(1)} %copy-done.73), kind=kOutput, calls=%fused_computation.15 | convolution fusion | flops 604569600 | bytes 3571712 | tf_op jit(solution)/shard_map/transpose(jvp())/dot_general | solution.py:72
  63.4 0.9 multiply_convert_fusion.6
  64.2 6.0 %fusion.110 = bf16[288,512]{1,0:T(8,128)(2,1)} fusion(bf16[2,512,2048]{2,1,0:T(8,128)(2,1)} %param.14, bf16[288,2048]{1,0:T(8,128)(2,1)} %convolution_convert_fusion.1, bf16[288,512]{1,0:T(8,128)(2,1)} %bitcast.247), kind=kOutput, calls=%fused_computation.118 | convolution fusion | flops 1219903488 | bytes 5963776 | tf_op jit(solution)/shard_map/transpose(jvp())/dot_general | solution.py:66
  70.3 1.5 fusion.145
  72.5 1.5 fusion.164
  74.0 1.6 add_add_fusion.11
  75.5 0.8 copy-done.18
  76.3 1.1 convolution_convert_fusion.13
  77.4 2.1 %reshape.505 = bf16[2,144,8,64]{3,2,1,0:T(8,128)(2,1)} reshape(bf16[288,512]{1,0:T(8,128)(2,1)} %convolution_convert_fusion.13) | data formatting | bytes 589824 | tf_op jit(solution)/shard_map/transpose(jvp())/reshape | solution.py:59
  79.5 2.2 %copy.161 = bf16[2,8,64,144]{3,2,1,0:T(8,128)(2,1)} copy(bf16[2,8,64,144]{2,1,3,0:T(8,128)(2,1)} %bitcast.241) | data formatting | bytes 589824 | tf_op jit(solution)/shard_map/transpose(jvp(whqk,wkhc->wqhc))/transpose | solution.py:55
  81.7 2.0 %fusion.89 = bf16[2,144,1,8,64]{1,4,3,0,2:T(8,128)(2,1)S(1)} fusion(bf16[2,8,64,144]{3,2,1,0:T(8,128)(2,1)} %copy.161, bf16[2,8,144,144]{2,3,1,0:T(8,128)(2,1)} %copy-done.7), kind=kOutput, calls=%fused_computation.109 | convolution fusion | flops 42614784 | bytes 1253376 | tf_op jit(solution)/shard_map/transpose(jvp(whqk,wkhc->wqhc))/dot_general | solution.py:55
  83.7 15.2 %fusion.11 = (f32[2,8,144]{2,1,0:T(8,128)S(1)}, bf16[2,8,144,144]{2,3,1,0:T(8,128)(2,1)S(1)}) fusion(f32[2,8,144,144]{2,3,1,0:T(8,128)} %copy-done.5, f32[2,8,144]{2,1,0:T(8,128)} %multiply_divide_fusion.1, f32[8]{0:T(128)S(1)} %copy-done.69, pred[2,144,144]{1,2,0:T(8,128)(4,1)S(1)} %copy-done.28, bf16[2,8,64,144]{3,2,1,0:T(8,128)(2,1)S(1)} %copy-done.20, ...), kind=kOutput, calls=%fused_computation.26 | convolution fusion | flops 44787456 | bytes 3131904 | tf_op jit(solution)/shard_map/transpose(jvp(whqk,wkhc->wqhc))/dot_general | solution.py:55
  99.0 1.0 fusion.84
  100.0 1.1 multiply_reduce_fusion.5
  101.7 1.4 pad_add_fusion.1
  103.1 3.0 %copy.166 = bf16[2,144,3,8,64]{4,3,2,1,0:T(8,128)(2,1)S(1)} copy(bf16[2,144,3,8,64]{1,4,3,0,2:T(8,128)(2,1)} %pad_add_fusion.1) | data formatting | bytes 1769472 | tf_op jit(solution)/shard_map/transpose(jvp())/add_any | solution.py:45
  106.1 1.1 reshape.506
  107.3 2.9 %multiply_reduce_fusion.11 = (f32[288]{0:T(512)}, f32[288,512]{1,0:T(8,128)S(1)}) fusion(f32[288,512]{1,0:T(8,128)S(1)} %copy-done.26, f32[512]{0:T(512)} %bitcast.260, f32[288]{0:T(512)} %div.176, bf16[288,1536]{1,0:T(8,128)(2,1)S(1)} %reshape.506, bf16[2,512,1536]{2,1,0:T(8,128)(2,1)} %param.12), kind=kOutput, calls=%fused_computation.185 | convolution fusion | flops 453721824 | bytes 3642496 | tf_op jit(solution)/shard_map/transpose(jvp())/dot_general | solution.py:39
  110.2 0.8 reduce_sum.279
  111.6 1.0 fusion.136
  113.4 0.9 fusion.135
  115.6 8.1 %collective-permute-done.4 = bf16[4,6,6,512]{3,2,1,0:T(8,128)(2,1)S(1)} collective-permute-done((bf16[4,6,6,512]{3,2,1,0:T(8,128)(2,1)S(1)}, bf16[4,6,6,512]{3,2,1,0:T(8,128)(2,1)S(1)}, u32[]{:S(2)}, u32[]{:S(2)}) %collective-permute-start.4) | collective-permute-done | bytes 147488 | tf_op jit(solution)/shard_map/ppermute | solution.py:17
  123.9 1.3 collective-permute-start.5
  125.2 6.5 %collective-permute-done.5 = bf16[4,3,12,512]{3,2,1,0:T(8,128)(2,1)S(1)} collective-permute-done((bf16[4,3,12,512]{3,2,1,0:T(8,128)(2,1)S(1)}, bf16[4,3,12,512]{3,2,1,0:T(8,128)(2,1)S(1)}, u32[]{:S(2)}, u32[]{:S(2)}) %collective-permute-start.5) | collective-permute-done | bytes 147488 | tf_op jit(solution)/shard_map/ppermute | solution.py:17
  132.0 3.4 %convolution_convert_fusion = bf16[288,2048]{1,0:T(8,128)(2,1)} fusion(bf16[288,512]{1,0:T(8,128)(2,1)S(1)} %reshape.509, bf16[2,2048,512]{2,1,0:T(8,128)(2,1)} %param.15), kind=kOutput, calls=%fused_computation.14 | convolution fusion | flops 603979776 | bytes 3571712 | tf_op jit(solution)/shard_map/transpose(jvp())/dot_general | solution.py:72
  135.4 5.3 %fusion.103 = bf16[288,512]{1,0:T(8,128)(2,1)S(1)} fusion(bf16[2,512,2048]{2,1,0:T(8,128)(2,1)} %param.14, bf16[288,2048]{1,0:T(8,128)(2,1)} %convolution_convert_fusion, bf16[288,512]{1,0:T(8,128)(2,1)S(1)} %bitcast.246), kind=kOutput, calls=%fused_computation.117 | convolution fusion | flops 1219903488 | bytes 5963776 | tf_op jit(solution)/shard_map/transpose(jvp())/dot_general | solution.py:66
  141.6 0.8 copy-done.16
  142.4 1.1 convolution_convert_fusion.12
  143.4 2.1 %reshape.513 = bf16[2,144,8,64]{3,2,1,0:T(8,128)(2,1)} reshape(bf16[288,512]{1,0:T(8,128)(2,1)} %convolution_convert_fusion.12) | data formatting | bytes 589824 | tf_op jit(solution)/shard_map/transpose(jvp())/reshape | solution.py:59
  145.5 2.2 %copy.181 = bf16[2,8,64,144]{3,2,1,0:T(8,128)(2,1)} copy(bf16[2,8,64,144]{2,1,3,0:T(8,128)(2,1)} %bitcast.242) | data formatting | bytes 589824 | tf_op jit(solution)/shard_map/transpose(jvp(whqk,wkhc->wqhc))/transpose | solution.py:55
  147.7 1.7 %fusion.90 = bf16[2,144,1,8,64]{1,4,3,0,2:T(8,128)(2,1)S(1)} fusion(bf16[2,8,64,144]{3,2,1,0:T(8,128)(2,1)} %copy.181, f32[2,8,144,144]{2,3,1,0:T(8,128)S(1)} %copy-done.9, f32[2,8,144]{2,1,0:T(8,128)S(1)} %copy-done.51), kind=kOutput, calls=%fused_computation.110 | convolution fusion | flops 43278336 | bytes 1926144 | tf_op jit(solution)/shard_map/transpose(jvp(whqk,wkhc->wqhc))/dot_general | solution.py:55
  152.7 1.4 pad_add_fusion
  154.1 2.9 %copy.186 = bf16[2,144,3,8,64]{4,3,2,1,0:T(8,128)(2,1)S(1)} copy(bf16[2,144,3,8,64]{1,4,3,0,2:T(8,128)(2,1)} %pad_add_fusion) | data formatting | bytes 1769472 | tf_op jit(solution)/shard_map/transpose(jvp())/add_any | solution.py:45
  157.1 1.9 %reshape.514 = bf16[288,1536]{1,0:T(8,128)(2,1)} reshape(bf16[2,144,3,8,64]{4,3,2,1,0:T(8,128)(2,1)S(1)} %copy.186) | data formatting | bytes 1769472 | tf_op jit(solution)/shard_map/transpose(jvp())/reshape | solution.py:44
  158.9 2.3 %fusion.100 = f32[288,512]{1,0:T(8,128)S(1)} fusion(bf16[288,1536]{1,0:T(8,128)(2,1)} %reshape.514, bf16[2,512,1536]{2,1,0:T(8,128)(2,1)} %param.12), kind=kOutput, calls=%fused_computation.114 | convolution fusion | flops 453132288 | bytes 3047424 | tf_op jit(solution)/shard_map/transpose(jvp())/dot_general | solution.py:39
  161.4 0.9 reshape.524
  162.3 1.4 multiply_reduce_fusion.8
  163.9 1.2 copy.192
  165.9 1.2 copy.191
  (250 shorter events, 29.1 us)
Async XLA Ops:
  0.6 9.3 %copy-start.10 = (bf16[4,6,12,512]{3,0,2,1:T(4,128)(2,1)S(1)}, bf16[4,6,12,512]{3,0,2,1:T(4,128)(2,1)}, u32[]{:S(2)}) copy-start(bf16[4,6,12,512]{3,0,2,1:T(4,128)(2,1)} %param.9) | copy-start | bytes 884740
  0.6 9.4 %copy-start.72 = (f32[2,8]{1,0:T(2,128)S(1)}, f32[2,8]{1,0:T(2,128)}, u32[]{:S(2)}) copy-start(f32[2,8]{1,0:T(2,128)} %param.17) | copy-start | bytes 196
  2.5 24.3 %collective-permute-start = (bf16[4,3,12,512]{3,0,2,1:T(4,128)(2,1)}, bf16[4,3,12,512]{3,0,2,1:T(4,128)(2,1)}, u32[]{:S(2)}, u32[]{:S(2)}) collective-permute-start(bf16[4,3,12,512]{3,0,2,1:T(4,128)(2,1)} %get-tuple-element.37), channel_id=1, source_target_pairs={{0,112},{16,0},{32,16},{48,32},{64,48},{80,64},{96,80},{112,96},{1... | collective-permute-start | bytes 442376 | tf_op jit(solution)/shard_map/ppermute | solution.py:17
  8.7 30.0 %collective-permute-start.2 = (bf16[4,3,12,512]{3,0,2,1:T(4,128)(2,1)}, bf16[4,3,12,512]{3,0,2,1:T(4,128)(2,1)}, u32[]{:S(2)}, u32[]{:S(2)}) collective-permute-start(bf16[4,3,12,512]{3,0,2,1:T(4,128)(2,1)} %get-tuple-element.33), channel_id=1, source_target_pairs={{0,112},{16,0},{32,16},{48,32},{64,48},{80,64},{96,80},{112,96},{1... | collective-permute-start | bytes 442376 | tf_op jit(solution)/shard_map/ppermute | solution.py:17
  11.7 3.8 %copy-start.64 = (f32[2,2,512]{2,1,0:T(2,128)S(1)}, f32[2,2,512]{2,1,0:T(2,128)}, u32[]{:S(2)}) copy-start(f32[2,2,512]{2,1,0:T(2,128)} %param.16) | copy-start | bytes 24580
  16.1 2.9 %copy-start.54 = (f32[1,1,512]{2,1,0:T(1,128)}, f32[1,1,512]{2,1,0:T(1,128)S(1)}, u32[]{:S(2)}) copy-start(f32[1,1,512]{2,1,0:T(1,128)S(1)} %get-tuple-element.43) | copy-start | bytes 6148
  16.1 8.4 %copy-start.12 = (f32[2,144,512]{2,1,0:T(8,128)}, f32[2,144,512]{2,1,0:T(8,128)S(1)}, u32[]{:S(2)}) copy-start(f32[2,144,512]{2,1,0:T(8,128)S(1)} %reshape.510) | copy-start | bytes 1769476
  21.0 1.4 copy-start.70
  22.0 1.6 copy-start
  22.3 1.4 copy-start.40
  22.3 1.4 copy-start.42
  22.4 1.3 copy-start.36
  22.4 1.3 copy-start.38
  23.1 1.4 copy-start.8
  23.7 1.5 copy-start.21
  24.6 2.2 %copy-start.30 = (bf16[4,3,12,512]{3,0,2,1:T(4,128)(2,1)S(1)}, bf16[4,3,12,512]{3,0,2,1:T(4,128)(2,1)}, u32[]{:S(2)}) copy-start(bf16[4,3,12,512]{3,0,2,1:T(4,128)(2,1)} %get-tuple-element.36) | copy-start | bytes 442372
  25.2 11.9 %copy-start.11 = (bf16[1536,512]{0,1:T(8,128)(2,1)S(1)}, bf16[1536,512]{0,1:T(8,128)(2,1)}, u32[]{:S(2)}) copy-start(bf16[1536,512]{0,1:T(8,128)(2,1)} %get-tuple-element.27) | copy-start | bytes 4718596
  25.7 9.4 %copy-start.56 = (f32[4,6,12]{2,0,1:T(4,128)S(1)}, f32[4,6,12]{2,0,1:T(4,128)}, u32[]{:S(2)}) copy-start(f32[4,6,12]{2,0,1:T(4,128)} %get-tuple-element.21) | copy-start | bytes 3460
  25.7 1.1 copy-start.48
  26.7 8.3 %copy-start.60 = (f32[2,144]{1,0:T(2,128)}, f32[2,144]{1,0:T(2,128)S(1)}, u32[]{:S(2)}) copy-start(f32[2,144]{1,0:T(2,128)S(1)} %multiply_reduce_fusion.10) | copy-start | bytes 3460
  27.9 10.8 %copy-start.29 = (bf16[4,3,12,512]{3,0,2,1:T(4,128)(2,1)S(1)}, bf16[4,3,12,512]{3,0,2,1:T(4,128)(2,1)}, u32[]{:S(2)}) copy-start(bf16[4,3,12,512]{3,0,2,1:T(4,128)(2,1)} %get-tuple-element.32) | copy-start | bytes 442372
  27.9 13.5 %collective-permute-start.1 = (bf16[4,6,6,512]{3,0,2,1:T(4,128)(2,1)S(1)}, bf16[4,6,6,512]{3,0,2,1:T(4,128)(2,1)S(1)}, u32[]{:S(2)}, u32[]{:S(2)}) collective-permute-start(bf16[4,6,6,512]{3,0,2,1:T(4,128)(2,1)S(1)} %get-tuple-element.35), channel_id=1, source_target_pairs={{0,15},{1,0},{2,1},{3,2},{4,3},{5,4},{6,5},{7,6},{8,7},{9,8},{10,9... | collective-permute-start | bytes 442376 | tf_op jit(solution)/shard_map/ppermute | solution.py:17
  39.8 4.2 %collective-permute-start.3 = (bf16[4,6,6,512]{3,0,2,1:T(4,128)(2,1)S(1)}, bf16[4,6,6,512]{3,0,2,1:T(4,128)(2,1)S(1)}, u32[]{:S(2)}, u32[]{:S(2)}) collective-permute-start(bf16[4,6,6,512]{3,0,2,1:T(4,128)(2,1)S(1)} %get-tuple-element.31), channel_id=1, source_target_pairs={{0,15},{1,0},{2,1},{3,2},{4,3},{5,4},{6,5},{7,6},{8,7},{9,8},{10,9... | collective-permute-start | bytes 442376 | tf_op jit(solution)/shard_map/ppermute | solution.py:17
  45.8 6.0 %copy-start.59 = (f32[1,1,512]{2,1,0:T(1,128)S(1)}, f32[1,1,512]{2,1,0:T(1,128)}, u32[]{:S(2)}) copy-start(f32[1,1,512]{2,1,0:T(1,128)} %get-tuple-element.42) | copy-start | bytes 6148
  52.9 3.4 %copy-start.28 = (pred[2,144,144]{1,2,0:T(8,128)(4,1)S(1)}, pred[2,144,144]{1,2,0:T(8,128)(4,1)}, u32[]{:S(2)}) copy-start(pred[2,144,144]{1,2,0:T(8,128)(4,1)} %broadcast_compare_fusion) | copy-start | bytes 124420
  52.9 3.4 %copy-start.68 = (f32[8]{0:T(128)S(1)}, f32[8]{0:T(128)}, u32[]{:S(2)}) copy-start(f32[8]{0:T(128)} %get-tuple-element.53) | copy-start | bytes 100
  56.3 1.6 copy-start.32
  57.2 1.7 %copy-start.5 = (f32[2,8,144,144]{2,3,1,0:T(8,128)}, f32[2,8,144,144]{2,3,1,0:T(8,128)S(1)}, u32[]{:S(2)}) copy-start(f32[2,8,144,144]{2,3,1,0:T(8,128)S(1)} %get-tuple-element.55) | copy-start | bytes 3981316
  57.9 1.2 copy-start.14
  57.9 1.5 copy-start.22
  58.5 1.4 copy-start.7
  58.5 1.7 %copy-start.31 = (bf16[288,512]{1,0:T(8,128)(2,1)S(1)}, bf16[288,512]{1,0:T(8,128)(2,1)}, u32[]{:S(2)}) copy-start(bf16[288,512]{1,0:T(8,128)(2,1)} %reshape.502) | copy-start | bytes 884740
  58.5 3.0 %copy-start.73 = (bf16[2,2048,512]{2,1,0:T(8,128)(2,1)S(1)}, bf16[2,2048,512]{2,1,0:T(8,128)(2,1)}, u32[]{:S(2)}) copy-start(bf16[2,2048,512]{2,1,0:T(8,128)(2,1)} %param.15) | copy-start | bytes 12582916
  59.9 3.5 %copy-start.4 = (f32[2,144,512]{2,1,0:T(8,128)}, f32[2,144,512]{2,1,0:T(8,128)S(1)}, u32[]{:S(2)}) copy-start(f32[2,144,512]{2,1,0:T(8,128)S(1)} %get-tuple-element.57) | copy-start | bytes 1769476
  59.9 3.4 %copy-start.53 = (f32[1,1,512]{2,1,0:T(1,128)S(1)}, f32[1,1,512]{2,1,0:T(1,128)}, u32[]{:S(2)}) copy-start(f32[1,1,512]{2,1,0:T(1,128)} %get-tuple-element.41) | copy-start | bytes 6148
  60.2 4.0 %copy-start.62 = (f32[2,144]{1,0:T(2,128)}, f32[2,144]{1,0:T(2,128)S(1)}, u32[]{:S(2)}) copy-start(f32[2,144]{1,0:T(2,128)S(1)} %multiply_reduce_fusion.12) | copy-start | bytes 3460
  61.6 2.7 %copy-start.58 = (f32[2,144]{1,0:T(2,128)}, f32[2,144]{1,0:T(2,128)S(1)}, u32[]{:S(2)}) copy-start(f32[2,144]{1,0:T(2,128)S(1)} %fusion.174) | copy-start | bytes 3460
  70.3 6.1 %copy-start.23 = (bf16[2,512,512]{2,1,0:T(8,128)(2,1)S(1)}, bf16[2,512,512]{2,1,0:T(8,128)(2,1)}, u32[]{:S(2)}) copy-start(bf16[2,512,512]{2,1,0:T(8,128)(2,1)} %param.13) | copy-start | bytes 3145732
  77.4 6.3 %copy-start.69 = (f32[8]{0:T(128)S(1)}, f32[8]{0:T(128)}, u32[]{:S(2)}) copy-start(f32[8]{0:T(128)} %get-tuple-element.53) | copy-start | bytes 100
  81.7 2.0 %copy-start.20 = (bf16[2,8,64,144]{3,2,1,0:T(8,128)(2,1)S(1)}, bf16[2,8,64,144]{3,2,1,0:T(8,128)(2,1)}, u32[]{:S(2)}) copy-start(bf16[2,8,64,144]{3,2,1,0:T(8,128)(2,1)} %copy.161) | copy-start | bytes 884740
  83.7 15.2 %copy-start.6 = (f32[2,8,144,144]{2,3,1,0:T(8,128)S(1)}, f32[2,8,144,144]{2,3,1,0:T(8,128)}, u32[]{:S(2)}) copy-start(f32[2,8,144,144]{2,3,1,0:T(8,128)} %copy-done.5) | copy-start | bytes 3981316
  83.7 15.2 %copy-start.35 = (f32[2,8,144]{2,1,0:T(8,128)S(1)}, f32[2,8,144]{2,1,0:T(8,128)}, u32[]{:S(2)}) copy-start(f32[2,8,144]{2,1,0:T(8,128)} %copy-done.34) | copy-start | bytes 27652
  100.0 1.1 copy-start.45
  100.0 1.1 copy-start.47
  103.1 4.1 %copy-start.26 = (f32[288,512]{1,0:T(8,128)S(1)}, f32[288,512]{1,0:T(8,128)}, u32[]{:S(2)}) copy-start(f32[288,512]{1,0:T(8,128)} %reshape.521) | copy-start | bytes 1769476
  107.3 6.1 %copy-start.15 = (f32[2,144,512]{2,1,0:T(8,128)S(1)}, f32[2,144,512]{2,1,0:T(8,128)}, u32[]{:S(2)}) copy-start(f32[2,144,512]{2,1,0:T(8,128)} %reshape.518) | copy-start | bytes 1769476
  107.3 6.1 %copy-start.19 = (f32[2,144,512]{2,1,0:T(8,128)S(1)}, f32[2,144,512]{2,1,0:T(8,128)}, u32[]{:S(2)}) copy-start(f32[2,144,512]{2,1,0:T(8,128)} %copy-done.18) | copy-start | bytes 1769476
  114.3 1.1 copy-start.3
  114.5 10.7 %copy-start.51 = (f32[2,8,144]{2,1,0:T(8,128)S(1)}, f32[2,8,144]{2,1,0:T(8,128)}, u32[]{:S(2)}) copy-start(f32[2,8,144]{2,1,0:T(8,128)} %copy-done.50) | copy-start | bytes 27652
  114.6 9.0 %collective-permute-start.4 = (bf16[4,6,6,512]{3,2,1,0:T(8,128)(2,1)S(1)}, bf16[4,6,6,512]{3,2,1,0:T(8,128)(2,1)S(1)}, u32[]{:S(2)}, u32[]{:S(2)}) collective-permute-start(bf16[4,6,6,512]{3,2,1,0:T(8,128)(2,1)S(1)} %fusion.157), channel_id=1, source_target_pairs={{0,1},{1,2},{2,3},{3,4},{4,5},{5,6},{6,7},{7,8},{8,9},{9,10},{10,1... | collective-permute-start | bytes 442376 | tf_op jit(solution)/shard_map/ppermute | solution.py:17
  123.9 7.8 %collective-permute-start.5 = (bf16[4,3,12,512]{3,2,1,0:T(8,128)(2,1)S(1)}, bf16[4,3,12,512]{3,2,1,0:T(8,128)(2,1)S(1)}, u32[]{:S(2)}, u32[]{:S(2)}) collective-permute-start(bf16[4,3,12,512]{3,2,1,0:T(8,128)(2,1)S(1)} %slice.335), channel_id=1, source_target_pairs={{0,16},{16,32},{32,48},{48,64},{64,80},{80,96},{96,112},{112,0},{1... | collective-permute-start | bytes 442376 | tf_op jit(solution)/shard_map/ppermute | solution.py:17
  135.4 5.5 %copy-start.61 = (f32[2,144]{1,0:T(2,128)S(1)}, f32[2,144]{1,0:T(2,128)}, u32[]{:S(2)}) copy-start(f32[2,144]{1,0:T(2,128)} %copy-done.60) | copy-start | bytes 3460
  140.6 1.7 %copy-start.24 = (bf16[2,512,512]{2,1,0:T(8,128)(2,1)S(1)}, bf16[2,512,512]{2,1,0:T(8,128)(2,1)}, u32[]{:S(2)}) copy-start(bf16[2,512,512]{2,1,0:T(8,128)(2,1)} %param.13) | copy-start | bytes 3145732
  141.5 6.2 %copy-start.9 = (f32[2,8,144,144]{2,3,1,0:T(8,128)S(1)}, f32[2,8,144,144]{2,3,1,0:T(8,128)}, u32[]{:S(2)}) copy-start(f32[2,8,144,144]{2,3,1,0:T(8,128)} %copy-done.8) | copy-start | bytes 3981316
  147.7 2.0 %copy-start.1 = (f32[2,144,3,8,64]{1,4,3,2,0:T(8,128)S(1)}, f32[2,144,3,8,64]{1,4,3,2,0:T(8,128)}, u32[]{:S(2)}) copy-start(f32[2,144,3,8,64]{1,4,3,2,0:T(8,128)} %copy-done) | copy-start | bytes 5308420
  147.7 2.1 %copy-start.27 = (bf16[2,8,64,144]{3,2,1,0:T(8,128)(2,1)S(1)}, bf16[2,8,64,144]{3,2,1,0:T(8,128)(2,1)}, u32[]{:S(2)}) copy-start(bf16[2,8,64,144]{3,2,1,0:T(8,128)(2,1)} %copy.181) | copy-start | bytes 884740
  158.9 3.4 %copy-start.55 = (f32[1,1,512]{2,1,0:T(1,128)S(1)}, f32[1,1,512]{2,1,0:T(1,128)}, u32[]{:S(2)}) copy-start(f32[1,1,512]{2,1,0:T(1,128)} %copy-done.54) | copy-start | bytes 6148
  161.3 3.8 %copy-start.66 = (f32[288]{0:T(512)S(1)}, f32[288]{0:T(512)}, u32[]{:S(2)}) copy-start(f32[288]{0:T(512)} %add.207) | copy-start | bytes 3460
  161.3 3.8 %copy-start.25 = (f32[288,512]{1,0:T(8,128)S(1)}, f32[288,512]{1,0:T(8,128)}, u32[]{:S(2)}) copy-start(f32[288,512]{1,0:T(8,128)} %reshape.515) | copy-start | bytes 1769476
  161.3 3.8 %copy-start.63 = (f32[288]{0:T(512)S(1)}, f32[288]{0:T(512)}, u32[]{:S(2)}) copy-start(f32[288]{0:T(512)} %div.199) | copy-start | bytes 3460
  161.3 4.2 %copy-start.65 = (f32[2,144]{1,0:T(2,128)S(1)}, f32[2,144]{1,0:T(2,128)}, u32[]{:S(2)}) copy-start(f32[2,144]{1,0:T(2,128)} %add.206) | copy-start | bytes 3460
  161.3 4.2 %copy-start.13 = (f32[2,144,512]{2,1,0:T(8,128)S(1)}, f32[2,144,512]{2,1,0:T(8,128)}, u32[]{:S(2)}) copy-start(f32[2,144,512]{2,1,0:T(8,128)} %copy-done.12) | copy-start | bytes 1769476
  161.3 4.2 %copy-start.17 = (f32[2,144,512]{2,1,0:T(8,128)S(1)}, f32[2,144,512]{2,1,0:T(8,128)}, u32[]{:S(2)}) copy-start(f32[2,144,512]{2,1,0:T(8,128)} %copy-done.16) | copy-start | bytes 1769476
  161.3 4.2 %copy-start.67 = (f32[2,144]{1,0:T(2,128)S(1)}, f32[2,144]{1,0:T(2,128)}, u32[]{:S(2)}) copy-start(f32[2,144]{1,0:T(2,128)} %div.196) | copy-start | bytes 3460
  (16 other events, 12.8 us)
where the time goes:
time: 168 us; the launch traced here: 167 us
  local copies, waits for them, and re-layouts  54.9 us (33%)
  matrix products  53.6 us (32%)
  other arithmetic  27.7 us (16%)
  waiting for transfers between devices  16.4 us (10%)
  starting transfers between devices  12.6 us (8%)
  between operations  2.04 us (1%)
    dot_general x6, matrix products, swin_block(): jnp.einsum('whqk,wkhc->wqhc', probabilities, values, preferred_element_ty...  20.2 us
    ppermute x6, waiting for transfers between devices, passed_along(): return lax.ppermute(value, axis, pairs)  16.4 us
    ppermute x6, starting transfers between devices, passed_along(): return lax.ppermute(value, axis, pairs)  12.6 us
    dot_general x2, matrix products, swin_block(): jnp.dot(normed_two.reshape(window_count * length, feature_width), w_upper...  11.3 us
    unnamed x150, local copies, waits for them, and re-layouts  10.4 us
    dot_general x4, matrix products, swin_block(): jnp.dot(normed.reshape(window_count * length, feature_width), w_in, prefe...  8.72 us
    dot_general x3, local copies, waits for them, and re-layouts, swin_block(): jnp.dot(normed.reshape(window_count * length, feature_width), w_in, prefe...  7.3 us
    add_any x2, local copies, waits for them, and re-layouts, swin_block(): queries = unit_rows(projected[:, :, 0]).astype(jnp.bfloat16)  5.9 us
  transfers between devices with their start and end apart: 6, of which 3 were waited for; matrix products, arithmetic and copies ran while one was open for 15% of the time, Pallas kernels for 0%

commit v1 on v0

v1 whole, which is shorter than its diff:
```python
import functools
import math

import jax
import jax.numpy as jnp
from jax import lax
from jax.experimental import pallas as pl
from jax.experimental.pallas import tpu as pltpu
from jax.sharding import PartitionSpec as P

F32 = jnp.float32
BF = jnp.bfloat16
MESH = pl.DeviceIdType.MESH

LV, RW, CL = 4, 6, 12
HR, HC = RW // 2, CL // 2
QT = HR * HC
NT = LV * RW * CL
WT = NT // 2
QN = LV * QT
D, FF, HEADS, HD = 512, 2048, 8, 64
PAIRS = HEADS // 2
EPS = 1e-05
QUADS = ((1, 1), (1, 0), (0, 1), (0, 0))
ORDER = ((0, 1, 2, 3), (1, 2, 3, 0))
QPAD = 80

C0 = math.sqrt(2.0 / math.pi)
C1 = 0.044715


def nn(a, b):
    return lax.dot_general(a, b, (((1,), (0,)), ((), ())), preferred_element_type=F32)


def nt(a, b):
    return lax.dot_general(a, b, (((1,), (1,)), ((), ())), preferred_element_type=F32)


def tn(a, b):
    return lax.dot_general(a, b, (((0,), (0,)), ((), ())), preferred_element_type=F32)


def row_chunks(size=48):
    return [slice(i, i + size) for i in range(0, NT, size)]


def kernel(
    lat_n, lon_n,
    x1_in, x2_in, ct_in, win_in, wout_in, wup_in, wdn_in, gains, scales,
    g1_out, g2_out,
    tiles, win, wout, wup, wdn,
    tmp, quad, xf, dyf, xh1, rstd1, xh2, rstd2, nb, qk, vv, rs, aa, rr, oo, gp,
    rf, dyb, du, dr, drb, dob, dqk, dp, dn, allow, bd, res,
    sbuf, rbuf, gsbuf, grbuf,
    in_sem, w_sem, out_sem, ssem, rsem,
):
    a = lax.axis_index("lat")
    b = lax.axis_index("lon")
    up, down = lax.rem(a + 1, lat_n), lax.rem(a + lat_n - 1, lat_n)
    east, west = lax.rem(b + 1, lon_n), lax.rem(b + lon_n - 1, lon_n)
    before = ((a, west), (down, b), (down, west))
    after = ((a, east), (up, b), (up, east))

    loads = [
        pltpu.make_async_copy(src, tiles.at[i], in_sem.at[i])
        for i, src in enumerate((x2_in, ct_in, x1_in))
    ]
    for c in loads:
        c.start()
    weights = {}
    for n, (name, blk) in enumerate(
        (("in", 0), ("out", 0), ("up", 0), ("in", 1), ("out", 1), ("up", 1), ("dn", 1), ("dn", 0))
    ):
        src, dst = {"in": (win_in, win), "out": (wout_in, wout), "up": (wup_in, wup), "dn": (wdn_in, wdn)}[name]
        weights[name, blk] = pltpu.make_async_copy(src.at[blk], dst.at[blk], w_sem.at[n])
        weights[name, blk].start()

    barrier = pltpu.get_barrier_semaphore()
    for dev in before + after:
        pl.semaphore_signal(barrier, inc=1, device_id=dev, device_id_type=MESH)

    def load_tile(i):
        loads[i].wait()
        tmp[...] = tiles[i].reshape(LV * RW, CL, D).astype(F32)

    def piece(lev, row, q):
        rq, cq = QUADS[q]
        return tmp[lev * RW + HR * rq + row, HC * cq:HC * cq + HC, :]

    def pack_out(i):
        load_tile(i)
        for q in (1, 2, 3):
            for m, lev in enumerate(ORDER[1]):
                for row in range(HR):
                    o = m * QT + row * HC
                    quad[q, o:o + HC, :] = piece(lev, row, q)
            sbuf[i, q - 1, 0:QN, :] = quad[q].astype(BF)

    def keep_own(dst):
        for m, lev in enumerate(ORDER[1]):
            w, h = divmod(m, 2)
            for row in range(HR):
                o = w * WT + h * QT + row * HC
                dst[o:o + HC, :] = piece(lev, row, 0)

    def send(i, src, dst, devs, base):
        out = []
        for j, dev in enumerate(devs):
            s = base + j
            c = pltpu.make_async_remote_copy(
                src_ref=src.at[j], dst_ref=dst.at[j], send_sem=ssem.at[s], recv_sem=rsem.at[s],
                device_id=dev, device_id_type=MESH,
            )
            c.start()
            out.append(c)
        return out

    pack_out(0)
    keep_own(xf.at[1])
    pl.semaphore_wait(barrier, 6)
    sent_x = send(0, sbuf.at[0], rbuf.at[0], before, 0)
    pack_out(1)
    keep_own(dyf.at[1])
    sent_c = send(1, sbuf.at[1], rbuf.at[1], before, 3)

    load_tile(2)
    for q in range(4):
        for m, lev in enumerate(ORDER[0]):
            w, h = divmod(m, 2)
            for row in range(HR):
                o = w * WT + q * 2 * QT + h * QT + row * HC
                xf[0, o:o + HC, :] = piece(lev, row, q)

    ri = lax.broadcasted_iota(jnp.int32, (256, 256), 0)
    ci = lax.broadcasted_iota(jnp.int32, (256, 256), 1)
    bd[...] = (lax.shift_right_logical(ri, 6) == lax.shift_right_logical(ci, 6)).astype(F32).astype(BF)
    last_band = (a == lat_n - 1).astype(jnp.int32)
    for w in range(2):
        labels = []
        for axis in (0, 1):
            t = lax.broadcasted_iota(jnp.int32, (WT, WT), axis)
            lab = 2 * last_band * (t >= 2 * 2 * QT).astype(jnp.int32)
            if w == 1:
                for step in range(1, 8):
                    sign = 1 if step % 2 else -1
                    lab = lab + sign * (t >= QT * step).astype(jnp.int32)
            labels.append(lab)
        allow[w] = (labels[0] == labels[1]).astype(F32)
    lane = lax.broadcasted_iota(jnp.int32, (WT, 128), 1)
    first_half = lane < HD
    m_a = first_half.astype(F32).astype(BF)
    m_b = (lane >= HD).astype(F32).astype(BF)
    ones = jnp.ones((WT, 128), BF)

    def stacked(v):
        return jnp.concatenate([v * m_a, v * m_b], axis=0)

    def wide(r):
        return jnp.concatenate([r, r[:, :WT - 128]], axis=1)

    def layer_norm(src, gain, xh, rstd):
        for s in row_chunks():
            x = src[s, :]
            c = x - jnp.mean(x, axis=-1, keepdims=True)
            inv = lax.rsqrt(jnp.mean(c * c, axis=-1, keepdims=True) + EPS)
            h = c * inv
            xh[s, :] = h
            rstd[s, :] = jnp.broadcast_to(inv, (h.shape[0], 128))
            nb[s, :] = (h * gain).astype(BF)

    def layer_norm_back(base, grad, gain, xh, rstd, dst, dst_bf=None):
        for s in row_chunks():
            g = grad[s, :] * gain
            h = xh[s, :]
            m1 = jnp.mean(g, axis=-1, keepdims=True)
            m2 = jnp.mean(g * h, axis=-1, keepdims=True)
            inv = rstd[s, 0:1]
            v = base[s, :] + inv * (g - m1 - h * m2)
            dst[s, :] = v
            if dst_bf is not None:
                dst_bf[s, :] = v.astype(BF)

    def forward(k):
        x = xf.at[k]
        layer_norm(x, gains[2 * k:2 * k + 1, :], xh1.at[k], rstd1.at[k])
        weights["in", k].wait()
        n1 = nb[...]
        for j in range(6):
            c = slice(256 * j, 256 * j + 256)
            p = nn(n1, win[k, :, c])
            if j < 4:
                inv = lax.rsqrt(nn((p * p).astype(BF), bd[...]) + 1e-06)
                rs[k, :, c] = inv
                qk[k, :, c] = (p * inv).astype(BF)
            else:
                vv[k, :, 256 * (j - 4):256 * (j - 4) + 256] = p.astype(BF)
        for w in range(2):
            rows = slice(WT * w, WT * w + WT)
            for pr in range(PAIRS):
                it = w * PAIRS + pr
                c = slice(128 * pr, 128 * pr + 128)
                ck = slice(D + 128 * pr, D + 128 * pr + 128)
                qs = stacked(qk[k, rows, c])
                s = nt(qs, qk[k, rows, ck])
                ea = jnp.exp(s[:WT] * scales[k, 2 * pr])
                eb = jnp.exp(s[WT:] * scales[k, 2 * pr + 1])
                if k == 1:
                    ea = ea * allow[w]
                    eb = eb * allow[w]
                e = jnp.concatenate([ea, eb], axis=0).astype(BF)
                aa[k, it] = e
                ou = nn(e, jnp.concatenate([vv[k, rows, c], ones], axis=1))
                r = 1.0 / ou[:, 128:]
                rr[k, it] = r
                on = ou[:, :128] * r
                oo[k, rows, c] = jnp.where(first_half, on[:WT], on[WT:]).astype(BF)
        weights["out", k].wait()
        o = oo[k]
        for j in range(2):
            c = slice(256 * j, 256 * j + 256)
            rf[:, c] = x[:, c] + nn(o, wout[k, :, c])
        layer_norm(rf, gains[2 * k + 1:2 * k + 2, :], xh2.at[k], rstd2.at[k])
        weights["up", k].wait()
        n2 = nb[...]
        for j in range(8):
            c = slice(256 * j, 256 * j + 256)
            u = nn(n2, wup[k, :, c])
            u2 = u * u
            t = jnp.tanh(u * (C0 + (C0 * C1) * u2))
            gp[k, :, c] = (0.5 + 0.5 * t) + (1.0 - t * t) * (u * (0.5 * C0 + (1.5 * C0 * C1) * u2))

    def backward(k):
        dy = dyf.at[k]
        for s in row_chunks():
            dyb[s, :] = dy[s, :].astype(BF)
        weights["dn", k].wait()
        g = dyb[...]
        for j in range(8):
            c = slice(256 * j, 256 * j + 256)
            du[:, c] = (nt(g, wdn[k, c, :]) * gp[k, :, c]).astype(BF)
        g = du[...]
        for j in range(2):
            c = slice(256 * j, 256 * j + 256)
            dn[:, c] = nt(g, wup[k, c, :])
        layer_norm_back(dy, dn, gains[2 * k + 1:2 * k + 2, :], xh2.at[k], rstd2.at[k], dr, drb)
        g = drb[...]
        for j in range(2):
            c = slice(256 * j, 256 * j + 256)
            dob[:, c] = nt(g, wout[k, c, :]).astype(BF)
        for w in range(2):
            rows = slice(WT * w, WT * w + WT)
            for pr in range(PAIRS):
                it = w * PAIRS + pr
                c = slice(128 * pr, 128 * pr + 128)
                ck = slice(D + 128 * pr, D + 128 * pr + 128)
                q, kk, v = qk[k, rows, c], qk[k, rows, ck], vv[k, rows, c]
                do = dob[rows, c]
                prod = do.astype(F32) * oo[k, rows, c].astype(F32)
                da = jnp.sum(jnp.where(first_half, prod, 0.0), axis=-1, keepdims=True)
                db = jnp.sum(jnp.where(first_half, 0.0, prod), axis=-1, keepdims=True)
                dos = stacked(do)
                dpr = nt(dos, v)
                e = aa[k, it]
                r = rr[k, it]
                ra = wide(r[:WT] * scales[k, 2 * pr])
                rb = wide(r[WT:] * scales[k, 2 * pr + 1])
                e32 = e.astype(F32)
                dsa = e32[:WT] * ra * (dpr[:WT] - da)
                dsb = e32[WT:] * rb * (dpr[WT:] - db)
                ds = jnp.concatenate([dsa, dsb], axis=0).astype(BF)
                dq = nn(ds, kk)
                dqk[rows, c] = jnp.where(first_half, dq[:WT], dq[WT:]).astype(BF)
                dqk[rows, ck] = tn(ds, stacked(q)).astype(BF)
                dor = (dos.astype(F32) * r).astype(BF)
                dp[rows, 2 * D + 128 * pr:2 * D + 128 * pr + 128] = tn(e, dor).astype(BF)
        for j in range(4):
            c = slice(256 * j, 256 * j + 256)
            g = dqk[:, c].astype(F32)
            h = qk[k, :, c].astype(F32)
            dot = nn((g * h).astype(BF), bd[...])
            dp[:, c] = (rs[k, :, c] * (g - h * dot)).astype(BF)
        g = dp[...]
        for j in range(2):
            c = slice(256 * j, 256 * j + 256)
            dn[:, c] = nt(g, win[k, c, :])
        layer_norm_back(dr, dn, gains[2 * k:2 * k + 1, :], xh1.at[k], rstd1.at[k], rf)

    forward(0)

    def unpack_in(i, copies, dst):
        for j, c in enumerate(copies):
            c.wait_recv()
            quad[j + 1] = rbuf[i, j, 0:QN, :].astype(F32)
            for w in range(2):
                o = w * WT + (j + 1) * 2 * QT
                dst[o:o + 2 * QT, :] = quad[j + 1, w * 2 * QT:(w + 1) * 2 * QT, :]

    unpack_in(0, sent_x, xf.at[1])
    forward(1)
    unpack_in(1, sent_c, dyf.at[1])
    backward(1)

    for q in range(4):
        for w in range(2):
            o = w * WT + q * 2 * QT
            quad[q, w * 2 * QT:(w + 1) * 2 * QT, :] = rf[o:o + 2 * QT, :]
        if q:
            gsbuf[q - 1, 0:QN, :] = quad[q].astype(BF)
    sent_g = send(2, gsbuf, grbuf, after, 6)
    for q in range(4):
        if q:
            sent_g[q - 1].wait_recv()
            quad[q] = grbuf[q - 1, 0:QN, :].astype(F32)
        rq, cq = QUADS[q]
        for m, lev in enumerate(ORDER[1]):
            for row in range(HR):
                o = m * QT + row * HC
                res[1, lev, HR * rq + row, HC * cq:HC * cq + HC, :] = quad[q, o:o + HC, :]
            w, h = divmod(lev, 2)
            o = w * WT + q * 2 * QT + h * QT
            dyf[0, o:o + QT, :] = quad[q, m * QT:(m + 1) * QT, :]
    out2 = pltpu.make_async_copy(res.at[1], g2_out, out_sem.at[1])
    out2.start()
    backward(0)
    for q in range(4):
        rq, cq = QUADS[q]
        for lev in range(LV):
            w, h = divmod(lev, 2)
            for row in range(HR):
                o = w * WT + q * 2 * QT + h * QT + row * HC
                res[0, lev, HR * rq + row, HC * cq:HC * cq + HC, :] = rf[o:o + HC, :]
    out1 = pltpu.make_async_copy(res.at[0], g1_out, out_sem.at[0])
    out1.start()
    for c in sent_x + sent_c + sent_g:
        c.wait_send()
    out2.wait()
    out1.wait()


def per_device(x_first, x_second, cotangent, w_attn_in, w_attn_out, w_up, w_down, norm_gains, logit_scales):
    any_spec = pl.BlockSpec(memory_space=pl.ANY)
    tile = (LV, RW, CL, D)
    v = pltpu.VMEM
    scratch = [
        v((3,) + tile, BF), v((2, D, 3 * D), BF), v((2, D, D), BF), v((2, D, FF), BF), v((2, FF, D), BF),
        v((LV * RW, CL, D), F32), v((4, QN, D), F32), v((2, NT, D), F32), v((2, NT, D), F32),
        v((2, NT, D), F32), v((2, NT, 128), F32), v((2, NT, D), F32), v((2, NT, 128), F32),
        v((NT, D), BF), v((2, NT, 2 * D), BF), v((2, NT, D), BF), v((2, NT, 2 * D), F32),
        v((2, 2 * PAIRS, 2 * WT, WT), BF), v((2, 2 * PAIRS, 2 * WT, 128), F32), v((2, NT, D), BF), v((2, NT, FF), F32),
        v((NT, D), F32), v((NT, D), BF), v((NT, FF), BF), v((NT, D), F32), v((NT, D), BF), v((NT, D), BF),
        v((NT, 2 * D), BF), v((NT, 3 * D), BF), v((NT, D), F32), v((2, WT, WT), F32), v((256, 256), BF),
        v((2,) + tile, F32),
        v((2, 3, QPAD, D), BF), v((2, 3, QPAD, D), BF), v((3, QPAD, D), BF), v((3, QPAD, D), BF),
        pltpu.SemaphoreType.DMA((3,)), pltpu.SemaphoreType.DMA((8,)), pltpu.SemaphoreType.DMA((2,)),
        pltpu.SemaphoreType.DMA((9,)), pltpu.SemaphoreType.DMA((9,)),
    ]
    body = functools.partial(kernel, lax.axis_size("lat"), lax.axis_size("lon"))
    return pl.pallas_call(
        body,
        out_shape=(jax.ShapeDtypeStruct(tile, F32), jax.ShapeDtypeStruct(tile, F32)),
        in_specs=[any_spec] * 7 + [pl.BlockSpec(memory_space=pltpu.VMEM), pl.BlockSpec(memory_space=pltpu.SMEM)],
        out_specs=(any_spec, any_spec),
        scratch_shapes=scratch,
        compiler_params=pltpu.CompilerParams(
            collective_id=0, has_side_effects=True, vmem_limit_bytes=60 * 1024 * 1024
        ),
        name="step",
    )(
        x_first, x_second, cotangent, w_attn_in, w_attn_out, w_up, w_down,
        norm_gains.reshape(4, D), logit_scales,
    )


def solution(mesh):
    grid = P(None, "lat", "lon", None)
    return jax.shard_map(
        per_device,
        mesh=mesh,
        in_specs=(grid, grid, grid, P(), P(), P(), P(), P(), P()),
        out_specs=(grid, grid),
        check_vma=False,
    )
```

time: 168 us -> 51.2 us (0.30)
  matrix products: 53.6 us -> 0 us
  local copies, waits for them, and re-layouts: 54.9 us -> 11.3 us
  Pallas kernels: 0 us -> 38.8 us
  other arithmetic: 27.7 us -> 0 us
  waiting for transfers between devices: 16.4 us -> 0 us
  starting transfers between devices: 12.6 us -> 0 us
    dot_general x24 -> x0, matrix products: 53.6 us -> none  [the longest x6 20.2 us: swin_block(): jnp.einsum('whqk,wkhc->wqhc', probabilities, values, preferred_element_ty...]
    pallas_call x0 -> x1, Pallas kernels: none -> 38.8 us  [per_device(): pl.pallas_call(body, out_shape=(jax.ShapeDtypeStruct(tile, F32), jax.Shap...]
    ppermute x6 -> x0, waiting for transfers between devices: 16.4 us -> none  [passed_along(): return lax.ppermute(value, axis, pairs)]
    ppermute x6 -> x0, starting transfers between devices: 12.6 us -> none  [passed_along(): return lax.ppermute(value, axis, pairs)]
    reduce_sum x15 -> x0, other arithmetic: 8.46 us -> none  [the longest x6 3.66 us: layer_norm(): center = tokens_in - jnp.mean(tokens_in, axis=-1, keepdims=True)]
    reshape x11 -> x1, local copies, waits for them, and re-layouts: 9.19 us -> 1.3 us  [per_device(): norm_gains.reshape(4, D)]
    dot_general x3 -> x0, local copies, waits for them, and re-layouts: 7.3 us -> none  [swin_block(): jnp.dot(normed.reshape(window_count * length, feature_width), w_in, prefe...]
    add_any x2 -> x0, local copies, waits for them, and re-layouts: 5.9 us -> none  [swin_block(): queries = unit_rows(projected[:, :, 0]).astype(jnp.bfloat16)]
  transfers between devices with their start and end apart: 6 -> 0, of which waited for: 3 -> 0; matrix products, arithmetic and copies ran while one was open for 15% -> 0% of each run, Pallas kernels for 0% -> 0%
where the time goes in v1:
time: 51.2 us; the launch traced here: 50.8 us
  Pallas kernels  38.8 us (76%)
  local copies, waits for them, and re-layouts  11.3 us (22%)
  between operations  0.64 us (1%)
    pallas_call x1, Pallas kernels, per_device(): pl.pallas_call(body, out_shape=(jax.ShapeDtypeStruct(tile, F32), jax.Shap...  38.8 us
    unnamed x3, local copies, waits for them, and re-layouts  5.33 us
    pallas_call x2, local copies, waits for them, and re-layouts, per_device(): pl.pallas_call(body, out_shape=(jax.ShapeDtypeStruct(tile, F32), jax.Shap...  4.66 us
    reshape x1, local copies, waits for them, and re-layouts, per_device(): norm_gains.reshape(4, D)  1.3 us

profile of v1, /device:TPU:0, one launch (start us, length us, event | category | flops | bytes accessed | tf_op | source)
XLA Modules:
  0.0 50.8 jit_solution(6732972294811234821)
XLA Ops:
  0.6 1.3 %reshape.7.gains = f32[4,512]{1,0:T(4,128)} reshape(f32[2,2,512]{2,1,0:T(2,128)} %param.16) | data formatting | bytes 16384 | tf_op jit(solution)/shard_map/reshape | solution.py:371
  1.9 1.8 %copy.11.x1_in = bf16[4,6,12,512]{3,2,1,0:T(8,128)(2,1)} copy(bf16[4,6,12,512]{3,0,2,1:T(4,128)(2,1)} %param.9) | data formatting | bytes 589824 | tf_op args[0]
  3.7 1.8 %copy.12.x2_in = bf16[4,6,12,512]{3,2,1,0:T(8,128)(2,1)} copy(bf16[4,6,12,512]{3,0,2,1:T(4,128)(2,1)} %param.10) | data formatting | bytes 589824 | tf_op args[1]
  5.5 1.8 %copy.13.ct_in = bf16[4,6,12,512]{3,2,1,0:T(8,128)(2,1)} copy(bf16[4,6,12,512]{3,0,2,1:T(4,128)(2,1)} %param.11) | data formatting | bytes 589824 | tf_op args[2]
  7.3 38.8 %step.1 = (f32[4,6,12,512]{3,2,1,0:T(8,128)}, f32[4,6,12,512]{3,2,1,0:T(8,128)}) custom-call(bf16[4,6,12,512]{3,2,1,0:T(8,128)(2,1)} %copy.11.x1_in, bf16[4,6,12,512]{3,2,1,0:T(8,128)(2,1)} %copy.12.x2_in, bf16[4,6,12,512]{3,2,1,0:T(8,128)(2,1)} %copy.13.ct_in, bf16[2,512,1536]{2,1,0:T(8,128)(2,1)} %win_in.1, bf16[2,512,512]{2,1,0:T(8,128)(2,1)} %wout_in.1, ...), custom_call_target="tpu_custom_call" | custom-call | tf_op jit(solution)/shard_map/step/pallas_call | solution.py:359
  46.1 2.3 %copy.14 = f32[4,6,12,512]{3,0,2,1:T(4,128)} copy(f32[4,6,12,512]{3,2,1,0:T(8,128)} %get-tuple-element.2) | data formatting | bytes 1179648 | tf_op jit(solution)/shard_map/step/pallas_call | solution.py:359
  48.4 2.3 %copy.15 = f32[4,6,12,512]{3,0,2,1:T(4,128)} copy(f32[4,6,12,512]{3,2,1,0:T(8,128)} %get-tuple-element.3) | data formatting | bytes 1179648 | tf_op jit(solution)/shard_map/step/pallas_call | solution.py:359

commit v2 on v1

--- a/solution.py
+++ b/solution.py
@@ -14,16 +14,14 @@
 
 LV, RW, CL = 4, 6, 12
 HR, HC = RW // 2, CL // 2
-QT = HR * HC
+RC = RW * CL
 NT = LV * RW * CL
 WT = NT // 2
-QN = LV * QT
 D, FF, HEADS, HD = 512, 2048, 8, 64
 PAIRS = HEADS // 2
 EPS = 1e-05
 QUADS = ((1, 1), (1, 0), (0, 1), (0, 0))
 ORDER = ((0, 1, 2, 3), (1, 2, 3, 0))
-QPAD = 80
 
 C0 = math.sqrt(2.0 / math.pi)
 C1 = 0.044715
@@ -50,9 +48,9 @@
     x1_in, x2_in, ct_in, win_in, wout_in, wup_in, wdn_in, gains, scales,
     g1_out, g2_out,
     tiles, win, wout, wup, wdn,
-    tmp, quad, xf, dyf, xh1, rstd1, xh2, rstd2, nb, qk, vv, rs, aa, rr, oo, gp,
+    moved, flat, xf, dyf, xh1, rstd1, xh2, rstd2, nb, qk, vv, rs, aa, rr, oo, gp,
     rf, dyb, du, dr, drb, dob, dqk, dp, dn, allow, bd, res,
-    sbuf, rbuf, gsbuf, grbuf,
+    gsend, grecv,
     in_sem, w_sem, out_sem, ssem, rsem,
 ):
     a = lax.axis_index("lat")
@@ -62,9 +60,16 @@
     before = ((a, west), (down, b), (down, west))
     after = ((a, east), (up, b), (up, east))
 
+    barrier = pltpu.get_barrier_semaphore()
+    for dev in before + after:
+        pl.semaphore_signal(barrier, inc=1, device_id=dev, device_id_type=MESH)
+
     loads = [
-        pltpu.make_async_copy(src, tiles.at[i], in_sem.at[i])
-        for i, src in enumerate((x2_in, ct_in, x1_in))
+        pltpu.make_async_copy(x2_in, tiles.at[0], in_sem.at[0]),
+        pltpu.make_async_copy(ct_in, tiles.at[1], in_sem.at[1]),
+        pltpu.make_async_copy(x1_in, tiles.at[2], in_sem.at[2]),
+        pltpu.make_async_copy(x2_in.at[HR:RW, HC:CL], moved.at[0, 0:HR, 0:HC], in_sem.at[3]),
+        pltpu.make_async_copy(ct_in.at[HR:RW, HC:CL], moved.at[1, 0:HR, 0:HC], in_sem.at[4]),
     ]
     for c in loads:
         c.start()
@@ -76,61 +81,59 @@
         weights[name, blk] = pltpu.make_async_copy(src.at[blk], dst.at[blk], w_sem.at[n])
         weights[name, blk].start()
 
-    barrier = pltpu.get_barrier_semaphore()
-    for dev in before + after:
-        pl.semaphore_signal(barrier, inc=1, device_id=dev, device_id_type=MESH)
-
-    def load_tile(i):
-        loads[i].wait()
-        tmp[...] = tiles[i].reshape(LV * RW, CL, D).astype(F32)
-
-    def piece(lev, row, q):
-        rq, cq = QUADS[q]
-        return tmp[lev * RW + HR * rq + row, HC * cq:HC * cq + HC, :]
-
-    def pack_out(i):
-        load_tile(i)
-        for q in (1, 2, 3):
-            for m, lev in enumerate(ORDER[1]):
-                for row in range(HR):
-                    o = m * QT + row * HC
-                    quad[q, o:o + HC, :] = piece(lev, row, q)
-            sbuf[i, q - 1, 0:QN, :] = quad[q].astype(BF)
-
-    def keep_own(dst):
-        for m, lev in enumerate(ORDER[1]):
-            w, h = divmod(m, 2)
-            for row in range(HR):
-                o = w * WT + h * QT + row * HC
-                dst[o:o + HC, :] = piece(lev, row, 0)
-
-    def send(i, src, dst, devs, base):
-        out = []
-        for j, dev in enumerate(devs):
-            s = base + j
-            c = pltpu.make_async_remote_copy(
-                src_ref=src.at[j], dst_ref=dst.at[j], send_sem=ssem.at[s], recv_sem=rsem.at[s],
-                device_id=dev, device_id_type=MESH,
-            )
-            c.start()
-            out.append(c)
-        return out
-
-    pack_out(0)
-    keep_own(xf.at[1])
+    def spots(half):
+        rq, cq = half
+        return [(r, c) for r in range(HR * rq, HR * rq + HR) for c in range(HC * cq, HC * cq + HC)]
+
+    def at(r, c):
+        o = LV * (r * CL + c)
+        return slice(o, o + LV)
+
+    def levels_apart(dst, order):
+        for m, lev in enumerate(order):
+            for j in range(D // 128):
+                dst[m * RC:m * RC + RC, 128 * j:128 * j + 128] = flat[j, pl.ds(lev, RC, stride=LV), :]
+
+    def levels_together(src, order):
+        for m, lev in enumerate(order):
+            for j in range(D // 128):
+                flat[j, pl.ds(lev, RC, stride=LV), :] = src[m * RC:m * RC + RC, 128 * j:128 * j + 128]
+
+    def set_flat(r, c, v):
+        for j in range(D // 128):
+            flat[j, at(r, c), :] = v[:, 128 * j:128 * j + 128]
+
+    def get_flat(r, c):
+        return jnp.concatenate([flat[j, at(r, c), :] for j in range(D // 128)], axis=1)
+
+    def from_tile(tile, dst, order):
+        for r in range(RW):
+            for c in range(CL):
+                set_flat(r, c, tile[r, c].astype(F32))
+        levels_apart(dst, order)
+
+    def block_of(ref, half):
+        rq, cq = half
+        return ref.at[HR * rq:HR * rq + HR, HC * cq:HC * cq + HC]
+
+    def swapped(half):
+        return (1 - half[0], 1 - half[1])
+
+    def send(src, dst, half, dev, n):
+        c = pltpu.make_async_remote_copy(
+            src_ref=block_of(src, half), dst_ref=block_of(dst, swapped(half)),
+            send_sem=ssem.at[n], recv_sem=rsem.at[n], device_id=dev, device_id_type=MESH,
+        )
+        c.start()
+        return c
+
+    loads[2].wait()
+    from_tile(tiles.at[2], xf.at[0], ORDER[0])
+    loads[0].wait()
     pl.semaphore_wait(barrier, 6)
-    sent_x = send(0, sbuf.at[0], rbuf.at[0], before, 0)
-    pack_out(1)
-    keep_own(dyf.at[1])
-    sent_c = send(1, sbuf.at[1], rbuf.at[1], before, 3)
-
-    load_tile(2)
-    for q in range(4):
-        for m, lev in enumerate(ORDER[0]):
-            w, h = divmod(m, 2)
-            for row in range(HR):
-                o = w * WT + q * 2 * QT + h * QT + row * HC
-                xf[0, o:o + HC, :] = piece(lev, row, q)
+    sent_x = [send(tiles.at[0], moved.at[0], QUADS[q], before[q - 1], q - 1) for q in (3, 2, 1)]
+    loads[1].wait()
+    sent_c = [send(tiles.at[1], moved.at[1], QUADS[q], before[q - 1], q + 2) for q in (3, 2, 1)]
 
     ri = lax.broadcasted_iota(jnp.int32, (256, 256), 0)
     ci = lax.broadcasted_iota(jnp.int32, (256, 256), 1)
@@ -140,11 +143,11 @@
         labels = []
         for axis in (0, 1):
             t = lax.broadcasted_iota(jnp.int32, (WT, WT), axis)
-            lab = 2 * last_band * (t >= 2 * 2 * QT).astype(jnp.int32)
+            second = (t >= RC).astype(jnp.int32)
+            late_rows = (t - RC * second >= RC // 2).astype(jnp.int32)
+            lab = 2 * last_band * late_rows
             if w == 1:
-                for step in range(1, 8):
-                    sign = 1 if step % 2 else -1
-                    lab = lab + sign * (t >= QT * step).astype(jnp.int32)
+                lab = lab + second
             labels.append(lab)
         allow[w] = (labels[0] == labels[1]).astype(F32)
     lane = lax.broadcasted_iota(jnp.int32, (WT, 128), 1)
@@ -183,7 +186,7 @@
 
     def forward(k):
         x = xf.at[k]
-        layer_norm(x, gains[2 * k:2 * k + 1, :], xh1.at[k], rstd1.at[k])
+        layer_norm(x, gains[k, 0:1, :], xh1.at[k], rstd1.at[k])
         weights["in", k].wait()
         n1 = nb[...]
         for j in range(6):
@@ -220,7 +223,7 @@
         for j in range(2):
             c = slice(256 * j, 256 * j + 256)
             rf[:, c] = x[:, c] + nn(o, wout[k, :, c])
-        layer_norm(rf, gains[2 * k + 1:2 * k + 2, :], xh2.at[k], rstd2.at[k])
+        layer_norm(rf, gains[k, 1:2, :], xh2.at[k], rstd2.at[k])
         weights["up", k].wait()
         n2 = nb[...]
         for j in range(8):
@@ -243,7 +246,7 @@
         for j in range(2):
             c = slice(256 * j, 256 * j + 256)
             dn[:, c] = nt(g, wup[k, c, :])
-        layer_norm_back(dy, dn, gains[2 * k + 1:2 * k + 2, :], xh2.at[k], rstd2.at[k], dr, drb)
+        layer_norm_back(dy, dn, gains[k, 1:2, :], xh2.at[k], rstd2.at[k], dr, drb)
         g = drb[...]
         for j in range(2):
             c = slice(256 * j, 256 * j + 256)
@@ -284,52 +287,47 @@
         for j in range(2):
             c = slice(256 * j, 256 * j + 256)
             dn[:, c] = nt(g, win[k, c, :])
-        layer_norm_back(dr, dn, gains[2 * k:2 * k + 1, :], xh1.at[k], rstd1.at[k], rf)
+        layer_norm_back(dr, dn, gains[k, 0:1, :], xh1.at[k], rstd1.at[k], rf)
 
     forward(0)
 
-    def unpack_in(i, copies, dst):
-        for j, c in enumerate(copies):
-            c.wait_recv()
-            quad[j + 1] = rbuf[i, j, 0:QN, :].astype(F32)
-            for w in range(2):
-                o = w * WT + (j + 1) * 2 * QT
-                dst[o:o + 2 * QT, :] = quad[j + 1, w * 2 * QT:(w + 1) * 2 * QT, :]
-
-    unpack_in(0, sent_x, xf.at[1])
+    loads[3].wait()
+    for c in sent_x:
+        c.wait_recv()
+    from_tile(moved.at[0], xf.at[1], ORDER[1])
     forward(1)
-    unpack_in(1, sent_c, dyf.at[1])
+    loads[4].wait()
+    for c in sent_c:
+        c.wait_recv()
+    from_tile(moved.at[1], dyf.at[1], ORDER[1])
     backward(1)
 
-    for q in range(4):
-        for w in range(2):
-            o = w * WT + q * 2 * QT
-            quad[q, w * 2 * QT:(w + 1) * 2 * QT, :] = rf[o:o + 2 * QT, :]
-        if q:
-            gsbuf[q - 1, 0:QN, :] = quad[q].astype(BF)
-    sent_g = send(2, gsbuf, grbuf, after, 6)
-    for q in range(4):
-        if q:
-            sent_g[q - 1].wait_recv()
-            quad[q] = grbuf[q - 1, 0:QN, :].astype(F32)
-        rq, cq = QUADS[q]
-        for m, lev in enumerate(ORDER[1]):
-            for row in range(HR):
-                o = m * QT + row * HC
-                res[1, lev, HR * rq + row, HC * cq:HC * cq + HC, :] = quad[q, o:o + HC, :]
-            w, h = divmod(lev, 2)
-            o = w * WT + q * 2 * QT + h * QT
-            dyf[0, o:o + QT, :] = quad[q, m * QT:(m + 1) * QT, :]
+    levels_together(rf, ORDER[1])
+    sent_g = []
+    for q in (3, 2, 1):
+        for r, c in spots(swapped(QUADS[q])):
+            gsend[r, c] = get_flat(r, c).astype(BF)
+    for q in (3, 2, 1):
+        sent_g.append(send(gsend, grecv, swapped(QUADS[q]), after[q - 1], q + 5))
+    own = {(r + HR, c + HC): get_flat(r, c) for r, c in spots((0, 0))}
+    for (r, c), v in own.items():
+        set_flat(r, c, v)
+        res[1, r, c] = v
+    for q, copy in zip((3, 2, 1), sent_g):
+        copy.wait_recv()
+    for q in (3, 2, 1):
+        for r, c in spots(QUADS[q]):
+            v = grecv[r, c].astype(F32)
+            set_flat(r, c, v)
+            res[1, r, c] = v
+    levels_apart(dyf.at[0], ORDER[0])
     out2 = pltpu.make_async_copy(res.at[1], g2_out, out_sem.at[1])
     out2.start()
     backward(0)
-    for q in range(4):
-        rq, cq = QUADS[q]
-        for lev in range(LV):
-            w, h = divmod(lev, 2)
-            for row in range(HR):
-                o = w * WT + q * 2 * QT + h * QT + row * HC
-                res[0, lev, HR * rq + row, HC * cq:HC * cq + HC, :] = rf[o:o + HC, :]
+    levels_together(rf, ORDER[0])
+    for r in range(RW):
+        for c in range(CL):
+            res[0, r, c] = get_flat(r, c)
     out1 = pltpu.make_async_copy(res.at[0], g1_out, out_sem.at[0])
     out1.start()
     for c in sent_x + sent_c + sent_g:
@@ -340,23 +338,24 @@
 
 def per_device(x_first, x_second, cotangent, w_attn_in, w_attn_out, w_up, w_down, norm_gains, logit_scales):
     any_spec = pl.BlockSpec(memory_space=pl.ANY)
-    tile = (LV, RW, CL, D)
+    tile = (RW, CL, LV, D)
     v = pltpu.VMEM
     scratch = [
         v((3,) + tile, BF), v((2, D, 3 * D), BF), v((2, D, D), BF), v((2, D, FF), BF), v((2, FF, D), BF),
-        v((LV * RW, CL, D), F32), v((4, QN, D), F32), v((2, NT, D), F32), v((2, NT, D), F32),
+        v((2,) + tile, BF), v((D // 128, NT, 128), F32), v((2, NT, D), F32), v((2, NT, D), F32),
         v((2, NT, D), F32), v((2, NT, 128), F32), v((2, NT, D), F32), v((2, NT, 128), F32),
         v((NT, D), BF), v((2, NT, 2 * D), BF), v((2, NT, D), BF), v((2, NT, 2 * D), F32),
         v((2, 2 * PAIRS, 2 * WT, WT), BF), v((2, 2 * PAIRS, 2 * WT, 128), F32), v((2, NT, D), BF), v((2, NT, FF), F32),
         v((NT, D), F32), v((NT, D), BF), v((NT, FF), BF), v((NT, D), F32), v((NT, D), BF), v((NT, D), BF),
         v((NT, 2 * D), BF), v((NT, 3 * D), BF), v((NT, D), F32), v((2, WT, WT), F32), v((256, 256), BF),
         v((2,) + tile, F32),
-        v((2, 3, QPAD, D), BF), v((2, 3, QPAD, D), BF), v((3, QPAD, D), BF), v((3, QPAD, D), BF),
-        pltpu.SemaphoreType.DMA((3,)), pltpu.SemaphoreType.DMA((8,)), pltpu.SemaphoreType.DMA((2,)),
+        v(tile, BF), v(tile, BF),
+        pltpu.SemaphoreType.DMA((5,)), pltpu.SemaphoreType.DMA((8,)), pltpu.SemaphoreType.DMA((2,)),
         pltpu.SemaphoreType.DMA((9,)), pltpu.SemaphoreType.DMA((9,)),
     ]
     body = functools.partial(kernel, lax.axis_size("lat"), lax.axis_size("lon"))
-    return pl.pallas_call(
+    cells = (1, 2, 0, 3)
+    out = pl.pallas_call(
         body,
         out_shape=(jax.ShapeDtypeStruct(tile, F32), jax.ShapeDtypeStruct(tile, F32)),
         in_specs=[any_spec] * 7 + [pl.BlockSpec(memory_space=pltpu.VMEM), pl.BlockSpec(memory_space=pltpu.SMEM)],
@@ -367,9 +366,10 @@
         ),
         name="step",
     )(
-        x_first, x_second, cotangent, w_attn_in, w_attn_out, w_up, w_down,
-        norm_gains.reshape(4, D), logit_scales,
+        *[jnp.transpose(v, cells) for v in (x_first, x_second, cotangent)],
+        w_attn_in, w_attn_out, w_up, w_down, norm_gains, logit_scales,
     )
+    return tuple(jnp.transpose(v, (2, 0, 1, 3)) for v in out)
 
 
 def solution(mesh):

time: 51.2 us -> 42.9 us (0.84)
  local copies, waits for them, and re-layouts: 11.3 us -> 3.88 us
  Pallas kernels: 38.8 us -> 38.1 us
    pallas_call x2 -> x0, local copies, waits for them, and re-layouts: 4.66 us -> none  [per_device(): pl.pallas_call(body, out_shape=(jax.ShapeDtypeStruct(tile, F32), jax.Shap...]
    unnamed x3 -> x2, local copies, waits for them, and re-layouts: 5.33 us -> 3.88 us
    reshape x1 -> x0, local copies, waits for them, and re-layouts: 1.3 us -> none  [per_device(): norm_gains.reshape(4, D)]
    pallas_call x1, Pallas kernels: 38.8 us -> 38.1 us  [per_device(): pl.pallas_call(body, out_shape=(jax.ShapeDtypeStruct(tile, F32), jax.Shap...]
where the time goes in v2:
time: 42.9 us; the launch traced here: 42.6 us
  Pallas kernels  38.1 us (89%)
  local copies, waits for them, and re-layouts  3.88 us (9%)
  between operations  0.64 us (1%)
    pallas_call x1, Pallas kernels, per_device(): pl.pallas_call(body, out_shape=(jax.ShapeDtypeStruct(tile, F32), jax.Shap...  38.1 us
    unnamed x2, local copies, waits for them, and re-layouts  3.88 us

profile of v2, /device:TPU:0, one launch (start us, length us, event | category | flops | bytes accessed | tf_op | source)
XLA Modules:
  0.0 42.6 jit_solution(9968593514717752396)
XLA Ops:
  0.6 38.1 %step.1 = (f32[6,12,4,512]{3,2,1,0:T(4,128)}, f32[6,12,4,512]{3,2,1,0:T(4,128)}) custom-call(bf16[6,12,4,512]{3,2,1,0:T(4,128)(2,1)} %bitcast.7, bf16[6,12,4,512]{3,2,1,0:T(4,128)(2,1)} %bitcast.8, bf16[6,12,4,512]{3,2,1,0:T(4,128)(2,1)} %bitcast.9, bf16[2,512,1536]{2,1,0:T(8,128)(2,1)} %win_in.1, bf16[2,512,512]{2,1,0:T(8,128)(2,1)} %wout_in.1, ...), custom_call_target="tpu_custom_call" | custom-call | tf_op jit(solution)/shard_map/step/pallas_call | solution.py:358
  38.8 1.9 %copy.13 = f32[4,6,12,512]{3,0,2,1:T(4,128)} copy(f32[4,6,12,512]{3,0,2,1:T(4,128)} %bitcast.6) | data formatting | bytes 1179648
  40.7 1.9 %copy.14 = f32[4,6,12,512]{3,0,2,1:T(4,128)} copy(f32[4,6,12,512]{3,0,2,1:T(4,128)} %bitcast.5) | data formatting | bytes 1179648

commit v3 on v2

--- a/solution.py
+++ b/solution.py
@@ -20,6 +20,7 @@
 D, FF, HEADS, HD = 512, 2048, 8, 64
 PAIRS = HEADS // 2
 EPS = 1e-05
+VMEM_LIMIT = 48 * 1024 * 1024
 QUADS = ((1, 1), (1, 0), (0, 1), (0, 0))
 ORDER = ((0, 1, 2, 3), (1, 2, 3, 0))
 
@@ -45,13 +46,13 @@
 
 def kernel(
     lat_n, lon_n,
-    x1_in, x2_in, ct_in, win_in, wout_in, wup_in, wdn_in, gains, scales,
+    x1_in, x2_in, ct_in, win_in, wout_in, wup_in, wdn_in, gains_in, scales_in,
     g1_out, g2_out,
     tiles, win, wout, wup, wdn,
     moved, flat, xf, dyf, xh1, rstd1, xh2, rstd2, nb, qk, vv, rs, aa, rr, oo, gp,
-    rf, dyb, du, dr, drb, dob, dqk, dp, dn, allow, bd, res,
-    gsend, grecv,
-    in_sem, w_sem, out_sem, ssem, rsem,
+    rf, dyb, du, dr, drb, dob, dqk, dp, dn, allow, bd,
+    gsend, grecv, gains, scales,
+    in_sem, w_sem, ssem, rsem,
 ):
     a = lax.axis_index("lat")
     b = lax.axis_index("lon")
@@ -70,16 +71,23 @@
         pltpu.make_async_copy(x1_in, tiles.at[2], in_sem.at[2]),
         pltpu.make_async_copy(x2_in.at[HR:RW, HC:CL], moved.at[0, 0:HR, 0:HC], in_sem.at[3]),
         pltpu.make_async_copy(ct_in.at[HR:RW, HC:CL], moved.at[1, 0:HR, 0:HC], in_sem.at[4]),
+        pltpu.make_async_copy(gains_in, gains, in_sem.at[5]),
+        pltpu.make_async_copy(scales_in, scales, in_sem.at[6]),
     ]
-    for c in loads:
-        c.start()
+    for i in (2, 0, 5, 6, 1, 3, 4):
+        loads[i].start()
     weights = {}
     for n, (name, blk) in enumerate(
         (("in", 0), ("out", 0), ("up", 0), ("in", 1), ("out", 1), ("up", 1), ("dn", 1), ("dn", 0))
     ):
         src, dst = {"in": (win_in, win), "out": (wout_in, wout), "up": (wup_in, wup), "dn": (wdn_in, wdn)}[name]
         weights[name, blk] = pltpu.make_async_copy(src.at[blk], dst.at[blk], w_sem.at[n])
-        weights[name, blk].start()
+
+    def fetch(*names):
+        for n in names:
+            weights[n].start()
+
+    fetch(("in", 0))
 
     def spots(half):
         rq, cq = half
@@ -130,6 +138,9 @@
     loads[2].wait()
     from_tile(tiles.at[2], xf.at[0], ORDER[0])
     loads[0].wait()
+    fetch(("out", 0), ("up", 0))
+    loads[5].wait()
+    loads[6].wait()
     pl.semaphore_wait(barrier, 6)
     sent_x = [send(tiles.at[0], moved.at[0], QUADS[q], before[q - 1], q - 1) for q in (3, 2, 1)]
     loads[1].wait()
@@ -188,6 +199,8 @@
         x = xf.at[k]
         layer_norm(x, gains[k, 0:1, :], xh1.at[k], rstd1.at[k])
         weights["in", k].wait()
+        if k == 0:
+            fetch(("in", 1), ("out", 1), ("up", 1))
         n1 = nb[...]
         for j in range(6):
             c = slice(256 * j, 256 * j + 256)
@@ -225,6 +238,8 @@
             rf[:, c] = x[:, c] + nn(o, wout[k, :, c])
         layer_norm(rf, gains[k, 1:2, :], xh2.at[k], rstd2.at[k])
         weights["up", k].wait()
+        if k == 0:
+            fetch(("dn", 1), ("dn", 0))
         n2 = nb[...]
         for j in range(8):
             c = slice(256 * j, 256 * j + 256)
@@ -312,32 +327,35 @@
     own = {(r + HR, c + HC): get_flat(r, c) for r, c in spots((0, 0))}
     for (r, c), v in own.items():
         set_flat(r, c, v)
-        res[1, r, c] = v
+        g2_out[r, c] = v
     for q, copy in zip((3, 2, 1), sent_g):
         copy.wait_recv()
     for q in (3, 2, 1):
         for r, c in spots(QUADS[q]):
             v = grecv[r, c].astype(F32)
             set_flat(r, c, v)
-            res[1, r, c] = v
+            g2_out[r, c] = v
     levels_apart(dyf.at[0], ORDER[0])
-    out2 = pltpu.make_async_copy(res.at[1], g2_out, out_sem.at[1])
-    out2.start()
     backward(0)
     levels_together(rf, ORDER[0])
     for r in range(RW):
         for c in range(CL):
-            res[0, r, c] = get_flat(r, c)
-    out1 = pltpu.make_async_copy(res.at[0], g1_out, out_sem.at[0])
-    out1.start()
+            g1_out[r, c] = get_flat(r, c)
     for c in sent_x + sent_c + sent_g:
         c.wait_send()
-    out2.wait()
-    out1.wait()
+
+
+def writer(a_ref, b_ref, a_out, b_out, sem):
+    copies = [pltpu.make_async_copy(a_ref, a_out, sem.at[0]), pltpu.make_async_copy(b_ref, b_out, sem.at[1])]
+    for c in copies:
+        c.start()
+    for c in copies:
+        c.wait()
 
 
 def per_device(x_first, x_second, cotangent, w_attn_in, w_attn_out, w_up, w_down, norm_gains, logit_scales):
-    any_spec = pl.BlockSpec(memory_space=pl.ANY)
+    any_spec = pl.BlockSpec(memory_space=pltpu.HBM)
+    vmem_spec = pl.BlockSpec(memory_space=pltpu.VMEM)
     tile = (RW, CL, LV, D)
     v = pltpu.VMEM
     scratch = [
@@ -348,9 +366,8 @@
         v((2, 2 * PAIRS, 2 * WT, WT), BF), v((2, 2 * PAIRS, 2 * WT, 128), F32), v((2, NT, D), BF), v((2, NT, FF), F32),
         v((NT, D), F32), v((NT, D), BF), v((NT, FF), BF), v((NT, D), F32), v((NT, D), BF), v((NT, D), BF),
         v((NT, 2 * D), BF), v((NT, 3 * D), BF), v((NT, D), F32), v((2, WT, WT), F32), v((256, 256), BF),
-        v((2,) + tile, F32),
-        v(tile, BF), v(tile, BF),
-        pltpu.SemaphoreType.DMA((5,)), pltpu.SemaphoreType.DMA((8,)), pltpu.SemaphoreType.DMA((2,)),
+        v(tile, BF), v(tile, BF), v((2, 2, D), F32), pltpu.SMEM((2, HEADS), F32),
+        pltpu.SemaphoreType.DMA((7,)), pltpu.SemaphoreType.DMA((8,)),
         pltpu.SemaphoreType.DMA((9,)), pltpu.SemaphoreType.DMA((9,)),
     ]
     body = functools.partial(kernel, lax.axis_size("lat"), lax.axis_size("lon"))
@@ -358,17 +375,26 @@
     out = pl.pallas_call(
         body,
         out_shape=(jax.ShapeDtypeStruct(tile, F32), jax.ShapeDtypeStruct(tile, F32)),
-        in_specs=[any_spec] * 7 + [pl.BlockSpec(memory_space=pltpu.VMEM), pl.BlockSpec(memory_space=pltpu.SMEM)],
-        out_specs=(any_spec, any_spec),
+        in_specs=[any_spec] * 9,
+        out_specs=(vmem_spec, vmem_spec),
         scratch_shapes=scratch,
         compiler_params=pltpu.CompilerParams(
-            collective_id=0, has_side_effects=True, vmem_limit_bytes=60 * 1024 * 1024
+            collective_id=0, has_side_effects=True, vmem_limit_bytes=VMEM_LIMIT
         ),
         name="step",
     )(
-        *[jnp.transpose(v, cells) for v in (x_first, x_second, cotangent)],
-        w_attn_in, w_attn_out, w_up, w_down, norm_gains, logit_scales,
+        *[pltpu.with_memory_space_constraint(v, pltpu.HBM) for v in [jnp.transpose(v, cells) for v in (x_first, x_second, cotangent)] + [
+        w_attn_in, w_attn_out, w_up, w_down, norm_gains, logit_scales]],
     )
+    out = pl.pallas_call(
+        writer,
+        out_shape=(jax.ShapeDtypeStruct(tile, F32), jax.ShapeDtypeStruct(tile, F32)),
+        in_specs=[vmem_spec, vmem_spec],
+        out_specs=(any_spec, any_spec),
+        scratch_shapes=[pltpu.SemaphoreType.DMA((2,))],
+        compiler_params=pltpu.CompilerParams(vmem_limit_bytes=4 * 1024 * 1024),
+        name="write",
+    )(*out)
     return tuple(jnp.transpose(v, (2, 0, 1, 3)) for v in out)
 
 

time: 42.9 us -> 38.5 us (0.90)
  local copies, waits for them, and re-layouts: 3.88 us -> 0 us
  Pallas kernels: 38.1 us -> 37.5 us
    unnamed x2 -> x0, local copies, waits for them, and re-layouts: 3.88 us -> none
    pallas_call x1, Pallas kernels: 38.1 us -> 36.5 us  [per_device(): pl.pallas_call(body, out_shape=(jax.ShapeDtypeStruct(tile, F32), jax.Shap...]
    pallas_call x0 -> x1, Pallas kernels: none -> 1.03 us  [per_device(): pl.pallas_call(writer, out_shape=(jax.ShapeDtypeStruct(tile, F32), jax.Sh...]
where the time goes in v3:
time: 38.5 us; the launch traced here: 38.3 us
  Pallas kernels  37.5 us (97%)
  between operations  0.8 us (2%)
    pallas_call x1, Pallas kernels, per_device(): pl.pallas_call(body, out_shape=(jax.ShapeDtypeStruct(tile, F32), jax.Shap...  36.5 us
    pallas_call x1, Pallas kernels, per_device(): pl.pallas_call(writer, out_shape=(jax.ShapeDtypeStruct(tile, F32), jax.Sh...  1.03 us

profile of v3, /device:TPU:0, one launch (start us, length us, event | category | flops | bytes accessed | tf_op | source)
XLA Modules:
  0.0 38.3 jit_solution(10976135668487244068)
XLA Ops:
  0.6 36.5 %step.1 = (f32[6,12,4,512]{3,2,1,0:T(4,128)S(1)}, f32[6,12,4,512]{3,2,1,0:T(4,128)S(1)}) custom-call(bf16[6,12,4,512]{3,2,1,0:T(4,128)(2,1)} %bitcast.5, bf16[6,12,4,512]{3,2,1,0:T(4,128)(2,1)} %bitcast.6, bf16[6,12,4,512]{3,2,1,0:T(4,128)(2,1)} %bitcast.7, bf16[2,512,1536]{2,1,0:T(8,128)(2,1)} %win_in.1, bf16[2,512,512]{2,1,0:T(8,128)(2,1)} %wout_in.1, ...), custom_call_target="tpu_custom_call" | custom-call | tf_op jit(solution)/shard_map/step/pallas_call | solution.py:375
  37.2 1.0 %write.1 = (f32[6,12,4,512]{3,2,1,0:T(4,128)}, f32[6,12,4,512]{3,2,1,0:T(4,128)}) custom-call(f32[6,12,4,512]{3,2,1,0:T(4,128)S(1)} %get-tuple-element.6.a_ref, f32[6,12,4,512]{3,2,1,0:T(4,128)S(1)} %get-tuple-element.7.b_ref), custom_call_target="tpu_custom_call" | custom-call | tf_op jit(solution)/shard_map/write/pallas_call | solution.py:389

commit v4 on v3

--- a/solution.py
+++ b/solution.py
@@ -21,6 +21,7 @@
 PAIRS = HEADS // 2
 EPS = 1e-05
 VMEM_LIMIT = 48 * 1024 * 1024
+FWD_DEPTH, BWD_DEPTH = 4, 4
 QUADS = ((1, 1), (1, 0), (0, 1), (0, 0))
 ORDER = ((0, 1, 2, 3), (1, 2, 3, 0))
 
@@ -38,6 +39,14 @@
 
 def tn(a, b):
     return lax.dot_general(a, b, (((0,), (0,)), ((), ())), preferred_element_type=F32)
+
+
+def pipelined(steps, depth):
+    waiting, active = list(steps), []
+    while waiting or active:
+        if waiting and len(active) < depth:
+            active.append(waiting.pop(0))
+        active = [g for g in active if next(g, active) is not active]
 
 
 def row_chunks(size=48):
@@ -74,7 +83,7 @@
         pltpu.make_async_copy(gains_in, gains, in_sem.at[5]),
         pltpu.make_async_copy(scales_in, scales, in_sem.at[6]),
     ]
-    for i in (2, 0, 5, 6, 1, 3, 4):
+    for i in (0, 2, 5, 6, 1, 3, 4):
         loads[i].start()
     weights = {}
     for n, (name, blk) in enumerate(
@@ -135,16 +144,20 @@
         c.start()
         return c
 
+    loads[0].wait()
+    pl.semaphore_wait(barrier, 6)
+    sent_x = [send(tiles.at[0], moved.at[0], QUADS[q], before[q - 1], q - 1) for q in (3, 2, 1)]
+    sent_c = []
+
+    def send_cotangent():
+        loads[1].wait()
+        sent_c.extend(send(tiles.at[1], moved.at[1], QUADS[q], before[q - 1], q + 2) for q in (3, 2, 1))
+
     loads[2].wait()
+    fetch(("out", 0), ("up", 0))
     from_tile(tiles.at[2], xf.at[0], ORDER[0])
-    loads[0].wait()
-    fetch(("out", 0), ("up", 0))
     loads[5].wait()
     loads[6].wait()
-    pl.semaphore_wait(barrier, 6)
-    sent_x = [send(tiles.at[0], moved.at[0], QUADS[q], before[q - 1], q - 1) for q in (3, 2, 1)]
-    loads[1].wait()
-    sent_c = [send(tiles.at[1], moved.at[1], QUADS[q], before[q - 1], q + 2) for q in (3, 2, 1)]
 
     ri = lax.broadcasted_iota(jnp.int32, (256, 256), 0)
     ci = lax.broadcasted_iota(jnp.int32, (256, 256), 1)
@@ -211,26 +224,31 @@
                 qk[k, :, c] = (p * inv).astype(BF)
             else:
                 vv[k, :, 256 * (j - 4):256 * (j - 4) + 256] = p.astype(BF)
-        for w in range(2):
+        def attend(w, pr):
             rows = slice(WT * w, WT * w + WT)
-            for pr in range(PAIRS):
-                it = w * PAIRS + pr
-                c = slice(128 * pr, 128 * pr + 128)
-                ck = slice(D + 128 * pr, D + 128 * pr + 128)
-                qs = stacked(qk[k, rows, c])
-                s = nt(qs, qk[k, rows, ck])
-                ea = jnp.exp(s[:WT] * scales[k, 2 * pr])
-                eb = jnp.exp(s[WT:] * scales[k, 2 * pr + 1])
-                if k == 1:
-                    ea = ea * allow[w]
-                    eb = eb * allow[w]
-                e = jnp.concatenate([ea, eb], axis=0).astype(BF)
-                aa[k, it] = e
-                ou = nn(e, jnp.concatenate([vv[k, rows, c], ones], axis=1))
-                r = 1.0 / ou[:, 128:]
-                rr[k, it] = r
-                on = ou[:, :128] * r
-                oo[k, rows, c] = jnp.where(first_half, on[:WT], on[WT:]).astype(BF)
+            it = w * PAIRS + pr
+            c = slice(128 * pr, 128 * pr + 128)
+            ck = slice(D + 128 * pr, D + 128 * pr + 128)
+            s = nt(stacked(qk[k, rows, c]), qk[k, rows, ck])
+            yield
+            ea = jnp.exp(s[:WT] * scales[k, 2 * pr])
+            eb = jnp.exp(s[WT:] * scales[k, 2 * pr + 1])
+            if k == 1:
+                ea = ea * allow[w]
+                eb = eb * allow[w]
+            e = jnp.concatenate([ea, eb], axis=0).astype(BF)
+            aa[k, it] = e
+            yield
+            ou = nn(e, jnp.concatenate([vv[k, rows, c], ones], axis=1))
+            yield
+            r = 1.0 / ou[:, 128:]
+            rr[k, it] = r
+            on = ou[:, :128] * r
+            oo[k, rows, c] = jnp.where(first_half, on[:WT], on[WT:]).astype(BF)
+
+        pipelined([attend(w, pr) for pr in range(PAIRS) for w in range(2)], FWD_DEPTH)
+        if k == 0:
+            send_cotangent()
         weights["out", k].wait()
         o = oo[k]
         for j in range(2):
@@ -243,7 +261,7 @@
         n2 = nb[...]
         for j in range(8):
             c = slice(256 * j, 256 * j + 256)
-            u = nn(n2, wup[k, :, c])
+            u = nn(n2, wup[k, :, c]).astype(BF)
             u2 = u * u
             t = jnp.tanh(u * (C0 + (C0 * C1) * u2))
             gp[k, :, c] = (0.5 + 0.5 * t) + (1.0 - t * t) * (u * (0.5 * C0 + (1.5 * C0 * C1) * u2))
@@ -256,7 +274,7 @@
         g = dyb[...]
         for j in range(8):
             c = slice(256 * j, 256 * j + 256)
-            du[:, c] = (nt(g, wdn[k, c, :]) * gp[k, :, c]).astype(BF)
+            du[:, c] = nt(g, wdn[k, c, :]).astype(BF) * gp[k, :, c]
         g = du[...]
         for j in range(2):
             c = slice(256 * j, 256 * j + 256)
@@ -266,32 +284,35 @@
         for j in range(2):
             c = slice(256 * j, 256 * j + 256)
             dob[:, c] = nt(g, wout[k, c, :]).astype(BF)
-        for w in range(2):
+        def attend_back(w, pr):
             rows = slice(WT * w, WT * w + WT)
-            for pr in range(PAIRS):
-                it = w * PAIRS + pr
-                c = slice(128 * pr, 128 * pr + 128)
-                ck = slice(D + 128 * pr, D + 128 * pr + 128)
-                q, kk, v = qk[k, rows, c], qk[k, rows, ck], vv[k, rows, c]
-                do = dob[rows, c]
-                prod = do.astype(F32) * oo[k, rows, c].astype(F32)
-                da = jnp.sum(jnp.where(first_half, prod, 0.0), axis=-1, keepdims=True)
-                db = jnp.sum(jnp.where(first_half, 0.0, prod), axis=-1, keepdims=True)
-                dos = stacked(do)
-                dpr = nt(dos, v)
-                e = aa[k, it]
-                r = rr[k, it]
-                ra = wide(r[:WT] * scales[k, 2 * pr])
-                rb = wide(r[WT:] * scales[k, 2 * pr + 1])
-                e32 = e.astype(F32)
-                dsa = e32[:WT] * ra * (dpr[:WT] - da)
-                dsb = e32[WT:] * rb * (dpr[WT:] - db)
-                ds = jnp.concatenate([dsa, dsb], axis=0).astype(BF)
-                dq = nn(ds, kk)
-                dqk[rows, c] = jnp.where(first_half, dq[:WT], dq[WT:]).astype(BF)
-                dqk[rows, ck] = tn(ds, stacked(q)).astype(BF)
-                dor = (dos.astype(F32) * r).astype(BF)
-                dp[rows, 2 * D + 128 * pr:2 * D + 128 * pr + 128] = tn(e, dor).astype(BF)
+            it = w * PAIRS + pr
+            c = slice(128 * pr, 128 * pr + 128)
+            ck = slice(D + 128 * pr, D + 128 * pr + 128)
+            do = dob[rows, c]
+            dos = stacked(do)
+            dpr = nt(dos, vv[k, rows, c])
+            prod = do.astype(F32) * oo[k, rows, c].astype(F32)
+            da = jnp.sum(jnp.where(first_half, prod, 0.0), axis=-1, keepdims=True)
+            db = jnp.sum(jnp.where(first_half, 0.0, prod), axis=-1, keepdims=True)
+            e = aa[k, it]
+            r = rr[k, it]
+            dor = (dos.astype(F32) * r).astype(BF)
+            dp[rows, 2 * D + 128 * pr:2 * D + 128 * pr + 128] = tn(e, dor).astype(BF)
+            yield
+            ra = wide(r[:WT] * scales[k, 2 * pr])
+            rb = wide(r[WT:] * scales[k, 2 * pr + 1])
+            e32 = e.astype(F32)
+            dsa = e32[:WT] * ra * (dpr[:WT] - da)
+            dsb = e32[WT:] * rb * (dpr[WT:] - db)
+            ds = jnp.concatenate([dsa, dsb], axis=0).astype(BF)
+            yield
+            dq = nn(ds, qk[k, rows, ck])
+            dqk[rows, ck] = tn(ds, stacked(qk[k, rows, c])).astype(BF)
+            yield
+            dqk[rows, c] = jnp.where(first_half, dq[:WT], dq[WT:]).astype(BF)
+
+        pipelined([attend_back(w, pr) for pr in range(PAIRS) for w in range(2)], BWD_DEPTH)
         for j in range(4):
             c = slice(256 * j, 256 * j + 256)
             g = dqk[:, c].astype(F32)
@@ -328,9 +349,8 @@
     for (r, c), v in own.items():
         set_flat(r, c, v)
         g2_out[r, c] = v
-    for q, copy in zip((3, 2, 1), sent_g):
-        copy.wait_recv()
-    for q in (3, 2, 1):
+    for q in (1, 2, 3):
+        sent_g[3 - q].wait_recv()
         for r, c in spots(QUADS[q]):
             v = grecv[r, c].astype(F32)
             set_flat(r, c, v)
@@ -363,7 +383,7 @@
         v((2,) + tile, BF), v((D // 128, NT, 128), F32), v((2, NT, D), F32), v((2, NT, D), F32),
         v((2, NT, D), F32), v((2, NT, 128), F32), v((2, NT, D), F32), v((2, NT, 128), F32),
         v((NT, D), BF), v((2, NT, 2 * D), BF), v((2, NT, D), BF), v((2, NT, 2 * D), F32),
-        v((2, 2 * PAIRS, 2 * WT, WT), BF), v((2, 2 * PAIRS, 2 * WT, 128), F32), v((2, NT, D), BF), v((2, NT, FF), F32),
+        v((2, 2 * PAIRS, 2 * WT, WT), BF), v((2, 2 * PAIRS, 2 * WT, 128), F32), v((2, NT, D), BF), v((2, NT, FF), BF),
         v((NT, D), F32), v((NT, D), BF), v((NT, FF), BF), v((NT, D), F32), v((NT, D), BF), v((NT, D), BF),
         v((NT, 2 * D), BF), v((NT, 3 * D), BF), v((NT, D), F32), v((2, WT, WT), F32), v((256, 256), BF),
         v(tile, BF), v(tile, BF), v((2, 2, D), F32), pltpu.SMEM((2, HEADS), F32),

time: 38.5 us -> 35.3 us (0.917)
  Pallas kernels: 37.5 us -> 34.4 us
    pallas_call x1, Pallas kernels: 36.5 us -> 33.4 us  [per_device(): pl.pallas_call(body, out_shape=(jax.ShapeDtypeStruct(tile, F32), jax.Shap...]
where the time goes in v4:
time: 35.3 us; the launch traced here: 35.2 us
  Pallas kernels  34.4 us (97%)
  between operations  0.8 us (2%)
    pallas_call x1, Pallas kernels, per_device(): pl.pallas_call(body, out_shape=(jax.ShapeDtypeStruct(tile, F32), jax.Shap...  33.4 us
    pallas_call x1, Pallas kernels, per_device(): pl.pallas_call(writer, out_shape=(jax.ShapeDtypeStruct(tile, F32), jax.Sh...  1.03 us

profile of v4, /device:TPU:0, one launch (start us, length us, event | category | flops | bytes accessed | tf_op | source)
XLA Modules:
  0.0 35.2 jit_solution(13167662256200716642)
XLA Ops:
  0.6 33.4 %step.1 = (f32[6,12,4,512]{3,2,1,0:T(4,128)S(1)}, f32[6,12,4,512]{3,2,1,0:T(4,128)S(1)}) custom-call(bf16[6,12,4,512]{3,2,1,0:T(4,128)(2,1)} %bitcast.5, bf16[6,12,4,512]{3,2,1,0:T(4,128)(2,1)} %bitcast.6, bf16[6,12,4,512]{3,2,1,0:T(4,128)(2,1)} %bitcast.7, bf16[2,512,1536]{2,1,0:T(8,128)(2,1)} %win_in.1, bf16[2,512,512]{2,1,0:T(8,128)(2,1)} %wout_in.1, ...), custom_call_target="tpu_custom_call" | custom-call | tf_op jit(solution)/shard_map/step/pallas_call | solution.py:395
  34.0 1.0 %write.1 = (f32[6,12,4,512]{3,2,1,0:T(4,128)}, f32[6,12,4,512]{3,2,1,0:T(4,128)}) custom-call(f32[6,12,4,512]{3,2,1,0:T(4,128)S(1)} %get-tuple-element.6.a_ref, f32[6,12,4,512]{3,2,1,0:T(4,128)S(1)} %get-tuple-element.7.b_ref), custom_call_target="tpu_custom_call" | custom-call | tf_op jit(solution)/shard_map/write/pallas_call | solution.py:409
